TPU v7x, 32 devices: a whole 2x2x4 slice. The times are simulated.
32 devices in a mesh: data: 32 (over z, y, x, core).
Axes of the slice: x: 2, y: 2, z: 4, core: 2. Of those that a mesh axis runs over, the one named last changes fastest.
Arguments:
- tokens: bfloat16 [262144, 384], P('data')
- out_grad: bfloat16 [262144, 384], P('data')
- w_up: bfloat16 [2, 384, 1536], replicated
- w_down: bfloat16 [2, 1536, 384], replicated
- a_up_old: float32 [2, 384, 384], replicated
- s_up_old: float32 [2, 1536, 1536], replicated
- a_down_old: float32 [2, 1536, 1536], replicated
- s_down_old: float32 [2, 384, 384], replicated
- a_up_inv: float32 [2, 384, 384], replicated
- s_up_inv: float32 [2, 1536, 1536], replicated
- a_down_inv: float32 [2, 1536, 1536], replicated
- s_down_inv: float32 [2, 384, 384], replicated
- factor_decay: float32 [], replicated
Outputs:
- output 1: float32 [2, 384, 1536], replicated
- output 2: float32 [2, 1536, 384], replicated
- output 3: float32 [2, 384, 384], replicated
- output 4: float32 [2, 1536, 1536], replicated
- output 5: float32 [2, 1536, 1536], replicated
- output 6: float32 [2, 384, 384], replicated
All inputs are finite; a program needn't handle non-finite values.
Results may differ from a plain program's by a relative error of at most 0.00153868.
Values are sent between devices in bfloat16 or wider.
A program may use at most 1 GiB of HBM per device.

v0:
```python
import functools

import jax
import jax.numpy as jnp
from jax import lax
from jax.experimental import pallas as pl
from jax.experimental.pallas import tpu as pltpu
from jax.sharding import PartitionSpec as P

bf16 = jnp.bfloat16
f32 = jnp.float32
D, FF, B = 384, 1536, 256
NB = FF // B
TRI = sum((j + 1) * B for j in range(NB))
NN = (((1,), (0,)), ((), ()))
NT = (((1,), (1,)), ((), ()))
TN = (((0,), (0,)), ((), ()))
TT = (((0,), (1,)), ((), ()))
GELU_K = 0.7978845608028654
GELU_C = 0.044715 * GELU_K
MIB = 1 << 20


def mm(left, right, dims):
    return lax.dot_general(left, right, dims, preferred_element_type=f32)


def half_sig(pre):
    cubic = GELU_C * (pre * pre)
    return 0.5 * jnp.tanh(pre * (cubic + GELU_K)) + 0.5, cubic


def gelu_back(pre, sig, cubic):
    hid = pre * sig
    return hid, sig + (hid * (1.0 - sig)) * (6.0 * cubic + 2.0 * GELU_K)


def add_tri(acc, mat):
    off = 0
    for j in range(NB):
        rows = (j + 1) * B
        acc[off:off + rows, :] += mm(mat[:rows, :], mat[j * B:rows, :], NT)
        off += rows


def add_small_tn(acc, rows):
    acc[0] += mm(rows[:, 0:128], rows[...], TN)
    acc[1, :, 0:256] += mm(rows[:, 128:256], rows[:, 128:384], TN)
    acc[1, :, 256:384] += mm(rows[:, 256:384], rows[:, 256:384], TN)


def add_small_nt(acc, cols):
    acc[0] += mm(cols[0:128, :], cols[...], NT)
    acc[1, :, 0:256] += mm(cols[128:256, :], cols[128:384, :], NT)
    acc[1, :, 256:384] += mm(cols[256:384, :], cols[256:384, :], NT)


def zero_first(accs):
    @pl.when(pl.program_id(0) == 0)
    def _():
        for acc in accs:
            acc[...] = jnp.zeros_like(acc)


MESH = pl.DeviceIdType.MESH
ORDER_X, ORDER_Y, ORDER_Z = (1, 2, 3, 4), (2, 1, 3, 4), (3, 4, 1, 2)
LINKS = {0: {0: 6e5}, 1: {1: 45e3}, 2: {2: 45e3}, 3: {3: 45e3}, 4: {3: 45e3, 4: 23e3}}
LAG = 2.5
SLACK = 3.0


def PRIORITY(f):
    return f.b


LAST = 10


def my_bits():
    me = lax.axis_index("data")
    bits = [(me // (1 << d)) % 2 for d in range(5)]
    return bits, [me + (1 - 2 * bits[d]) * (1 << d) for d in range(5)]


def entry_barrier():
    peers = my_bits()[1]
    barrier = pltpu.get_barrier_semaphore()
    for peer in peers:
        pl.semaphore_signal(barrier, inc=1, device_id=(peer,), device_id_type=MESH)
    pl.semaphore_wait(barrier, len(peers))


def al(row):
    return pl.multiple_of(row, 8)


class Flow:
    def __init__(self, name, row0, rows, cols, order, shard_row, wide):
        self.name, self.row0, self.rows, self.cols, self.order = name, row0, rows, cols, order
        self.shard_row, self.wide = shard_row, wide
        self.at, self.start = 0, 0.0
        self.part = name + ":part%d" % row0

    def fan(self):
        other = Flow(self.name, self.row0, self.rows, self.cols, self.order, self.shard_row, True)
        other.at = 5
        return other

    def dim(self, s):
        if s in (0, LAST - 1):
            return 0
        return self.order[s - 1] if s < 5 else self.order[LAST - 2 - s]

    def length(self, s):
        return self.rows >> s if s < 5 else self.rows >> (LAST - 1 - s)

    def kept(self, steps):
        return self.rows >> (steps - 1)

    def open(self, a, b):
        self.a, self.b = a, b
        n = b - a
        out = [pltpu.SemaphoreType.DMA((2,)), pltpu.SemaphoreType.DMA((n,)), pltpu.SemaphoreType.DMA((n,))]
        if a < 5:
            out.append(pltpu.VMEM((self.rows if a == 0 else self.kept(a), self.cols), f32))
            out.append(pltpu.VMEM((sum(self.length(s) for s in range(a, min(b, 5))), self.cols), f32))
        elif a == 5 and not self.wide:
            out.append(pltpu.VMEM((self.kept(5), self.cols), f32))
        return out

    def bind(self, named, scr):
        a, b, row0, rows = self.a, self.b, self.row0, self.rows
        sem_l, sem_s, sem_r = scr[:3]
        bits, peers = my_bits()
        core = bits[0]
        lens, offs = [rows], [0]
        for d in self.order:
            lens.append(lens[-1] // 2)
            offs.append(offs[-1] + bits[d] * lens[-1])
        src, dst = named.get(self.name + ":src"), named.get(self.name + ":dst")
        part_in, part_out = named.get(self.part + ":in"), named.get(self.part + ":out")
        base = offs[min(max(a, 1), 5) - 1]
        work = recv = None
        if a < 5:
            work, recv = scr[3:]
        elif a == 5:
            work = named[self.name + ":first"].at[pl.ds(self.shard_row, 8), :] if self.wide else scr[3]
        sends, begin_recv, locals_ = {}, {}, []

        def remote(s, x, y):
            return pltpu.make_async_remote_copy(src_ref=x, dst_ref=y, send_sem=sem_s.at[s - a], recv_sem=sem_r.at[s - a],
                                                device_id=(peers[self.dim(s)],), device_id_type=MESH)

        def final():
            return work if a == 5 else work.at[pl.ds(al(offs[4] - base), lens[4]), :]

        def spot(k):
            return dst.at[core, pl.ds(al(row0 + offs[k]), lens[k]), :]

        at = 0
        for s in range(a, b):
            if s < 5:
                begin_recv[s] = at
                to = recv.at[pl.ds(at, self.length(s)), :]
                at += self.length(s)
                if s == 0:
                    sends[s] = remote(s, src.at[1 - core, pl.ds(row0, rows), :], to)
                else:
                    gone = al(offs[s - 1] - base + (1 - bits[self.dim(s)]) * lens[s])
                    sends[s] = remote(s, work.at[pl.ds(gone, lens[s]), :], to)
            else:
                k = LAST - 1 - s
                sends[s] = remote(s, final() if s == 5 else spot(k), spot(k))
        load = place = save = None
        if a == 0:
            load = pltpu.make_async_copy(src.at[core, pl.ds(row0, rows), :], work, sem_l.at[0])
        elif a < 5 or (a == 5 and not self.wide):
            load = pltpu.make_async_copy(part_in, work, sem_l.at[0])
        if a <= 5 < b:
            place = pltpu.make_async_copy(final(), spot(4), sem_l.at[1])
        if b <= 5:
            kept = work.at[pl.ds(al(offs[b - 1] - base), lens[b - 1]), :]
            save = pltpu.make_async_copy(kept, part_out, sem_l.at[1])

        def add(row, frm, count):
            for q in range(0, count, 64):
                step = min(count - q, 64)
                x, y = al(row + q), al(frm + q)
                work[pl.ds(x, step), :] = work[pl.ds(x, step), :] + recv[pl.ds(y, step), :]

        def take(s, then):
            if s == a and load is not None and a == 0:
                load.wait()
            sends[s].wait_recv()
            if s == 5 and place is not None:
                place.wait()
            if s >= 5:
                then()
            elif s == 4 or s + 1 == b:
                add(offs[s] - base, begin_recv[s], lens[s])
                then()
            else:
                half = lens[s + 1]
                bit = bits[self.dim(s + 1)]
                add(offs[s] - base + (1 - bit) * half, begin_recv[s] + (1 - bit) * half, half)
                then()
                add(offs[s] - base + bit * half, begin_recv[s] + bit * half, half)

        def send(s):
            if s == 5:
                place.start()
            sends[s].start()

        def begin():
            load.start()
            if a == 0:
                send(0)

        def go(s):
            if s > a:
                take(s - 1, lambda: send(s))
            else:
                if load is not None:
                    load.wait()
                send(s)

        def stop():
            take(b - 1, save.start if save is not None else lambda: None)

        def end():
            if save is not None:
                save.wait()
            for s in range(a, b):
                sends[s].wait_send()

        return {"begin": begin, "go": go, "stop": lambda s: stop(), "end": end}


class First:
    def __init__(self, name, flows, inverse, block):
        self.name, self.flows, self.inverse, self.block, self.done = name, flows, inverse, block, False
        self.fans = [f.fan() for f in flows]

    def open(self):
        rows = pltpu.VMEM((24, 768), f32)
        return [pltpu.SemaphoreType.DMA((4,)), pltpu.SemaphoreType.DMA((3,)), pltpu.SemaphoreType.DMA((3,)),
                rows, rows, rows, pltpu.VMEM((FF, 768), f32)]

    def bind(self, named, scr):
        sem_l, sem_s, sem_r, own, other, prod, inv_v = scr
        named[self.name + ":first"] = prod
        bits, peers = my_bits()
        core = bits[0]
        inv = named[self.name + ":inv"]
        copies, swaps = [], []
        for i, flow in enumerate(self.flows):
            rows = named.get(flow.part + ":out", named.get(flow.part + ":in"))
            spot = pl.ds(flow.shard_row, 8)
            copies.append(pltpu.make_async_copy(rows, own.at[spot, :], sem_l.at[i]))
            swaps.append(pltpu.make_async_remote_copy(
                src_ref=rows, dst_ref=other.at[spot, :], send_sem=sem_s.at[i], recv_sem=sem_r.at[i],
                device_id=(peers[0],), device_id_type=MESH))
        copies.append(pltpu.make_async_copy(
            inv.at[self.block, :, pl.ds(pl.multiple_of(core * 768, 128), 768)], inv_v, sem_l.at[3]))

        def begin():
            for copy in copies + swaps:
                copy.start()

        def go(s):
            for copy in copies + swaps:
                copy.wait()
            prod[...] = (precise(own[...], inv_v[pl.ds(al(core * 768), 768), :])
                         + precise(other[...], inv_v[pl.ds(al((1 - core) * 768), 768), :]))

        return {"begin": begin, "go": go}


def plan(flows, firsts, tick_us, last, over=4.0):
    times = [0.0]
    for us in tick_us:
        times.append(times[-1] + us)
    limit = 1e9 if last else times[-1]
    free, now_rest = {}, times[-1]
    slots, rest = [[] for _ in tick_us], []
    ready = {f: f.start for f in flows}
    phase = {f: "new" for f in flows}
    for f in flows:
        f.a = f.b = f.at
    fstate = {f: "new" for f in firsts}
    fready = {}

    def arrival(f, s, now):
        links = LINKS[f.dim(s)]
        size = f.length(s) * f.cols * 4
        begin = max([now] + [free.get(link, 0.0) for link in links])
        return begin, max(begin + size / rate for rate in links.values()), size

    def send(f, s, now):
        begin, end, size = arrival(f, s, now)
        for link, rate in LINKS[f.dim(s)].items():
            free[link] = begin + size / rate
        f.b = s + 1
        ready[f] = end + LAG

    def allowed(f, s, now):
        return last or (now < limit and arrival(f, s, now)[1] + LAG < limit + over)

    def clear(f, s, now):
        return arrival(f, s, now)[0] <= now + SLACK

    def move(f, now):
        if ready[f] > now:
            return None
        if phase[f] == "new":
            if f.at >= LAST or f.wide and f.at == 5:
                return None
            if not allowed(f, f.at, now + (LAG if 0 < f.at <= 5 else 0.0)):
                return None
            if not clear(f, f.at, now):
                return None
            if f.at == 0:
                phase[f] = "run"
                send(f, 0, now)
                return "begin", 0
            if f.at <= 5:
                phase[f] = "loaded"
                ready[f] = now + LAG
                f.b = f.at + 1
                return "begin", 0
            phase[f] = "run"
            send(f, f.at, now)
            return "go", f.at
        if phase[f] == "loaded":
            phase[f] = "run"
            send(f, f.at, now)
            return "go", f.at
        if phase[f] == "run":
            s = f.b
            if s == LAST or f.wide and s == 5 or not allowed(f, s, now):
                phase[f] = "saved"
                ready[f] = now + LAG
                return "stop", s
            if not clear(f, s, now):
                return None
            send(f, s, now)
            return "go", s
        if phase[f] == "saved":
            phase[f] = "done"
            return "end", 0
        return None

    def first_move(f, now):
        if f.done or fready.get(f, 0.0) > now:
            return None
        if fstate[f] == "new":
            ok = all(x.b == 5 and phase.get(x, "done") in ("new", "done") for x in f.flows)
            if not ok or not (last or now + 20.0 < limit):
                return None
            fstate[f] = "loaded"
            fready[f] = now + 5.0
            return "begin", 0
        if fstate[f] == "loaded":
            fstate[f] = "done"
            return "go", 0
        return None

    def sweep(now, out):
        again = True
        while again:
            again = False
            for f in sorted(flows, key=PRIORITY):
                e = move(f, now)
                if e:
                    out.append((f,) + e)
                    again = True
                    break
            for f in firsts:
                e = first_move(f, now)
                if e:
                    out.append((f,) + e)
                    again = True
                    if fstate[f] == "done":
                        for x in f.fans:
                            flows.append(x)
                            x.a = 5
                            phase[x] = "run"
                            send(x, 5, now)
                            out.append((x, "go", 5))

    for t, now in enumerate(times[:-1]):
        sweep(now, slots[t])
    now = times[-1]
    while True:
        sweep(now, rest)
        later = [ready[f] for f in flows if phase[f] in ("loaded", "run", "saved") and ready[f] > now]
        later += [fready[f] for f in firsts if fstate[f] == "loaded" and fready[f] > now]
        held = any(phase[f] in ("loaded", "run") or last and phase[f] == "new" and f.at < LAST and not (f.wide and f.at == 5)
                   for f in flows)
        if not later and not held:
            return slots, rest, now
        now = min(later + ([now + 1.0] if held else []))


def tri_col(acc, mat, j):
    rows = (j + 1) * B
    off = B * j * (j + 1) // 2
    acc[off:off + rows, :] += mm(mat[:rows, :], mat[j * B:rows, :], NT)


def staged(dot, act, backs, shifts, accs, setup=None):
    step, last = pl.program_id(0), pl.num_programs(0) - 1

    def shift():
        for old, new in shifts:
            old[...] = new[...]

    @pl.when(step == 0)
    def _():
        for acc in accs:
            acc[...] = jnp.zeros_like(acc)
        if setup is not None:
            setup()
        for k in range(NB):
            act(k, dot(k))

    @pl.when((step > 0) & (step < last))
    def _():
        shift()
        for k, back in enumerate(backs):
            value = dot(k)
            back()
            act(k, value)

    @pl.when(step == last)
    def _():
        shift()
        for back in backs:
            back()


def block(k):
    return slice(k * B, (k + 1) * B)


def tri_pieces(acc, mat, *more):
    pieces = [(5,), (4,), (3, 0), (2, 1)]

    def run(cols, fns):
        for j in cols:
            tri_col(acc, mat, j)
        for fn in fns:
            fn()

    return [functools.partial(run, cols, ()) for cols in pieces] + [functools.partial(run, (), fns) for fns in more]


def gelu_act(pre_out, new_s):
    def act(k, value):
        pre = value.astype(bf16)
        pre_out[block(k), :] = pre
        pre = pre.astype(f32)
        new_s[block(k), :] = (pre * half_sig(pre)[0]).astype(bf16)
    return act


def stage1(tok, grad, w_up, w_down, tok_b, grad_b, pre_out, next_out, tri, small_u, small_q, new_s, hid_s, up_s, down_s):
    def setup():
        up_s[...] = w_up[0].T
        down_s[...] = w_down[0].T

    def dot(k):
        return mm(up_s[block(k), :], tok[...], NT)

    def down():
        next_out[...] = mm(down_s[...], hid_s[...], NN).astype(bf16)

    backs = tri_pieces(tri, hid_s, (down,), (lambda: add_small_tn(small_u, tok_b), lambda: add_small_tn(small_q, grad_b)))
    staged(dot, gelu_act(pre_out, new_s), backs, ((hid_s, new_s),), (tri, small_u, small_q), setup)


def add_wide(acc, left, mat, dims, h):
    acc[h] += mm(left[...], mat[h * FF // 2:(h + 1) * FF // 2, :], dims)


def stage2(u_t, w_up, u_b, grad_b, pre_out, tri, small_u, dwd, new_s, hid_s, up_s):
    def setup():
        up_s[...] = w_up[0].T

    def dot(k):
        return mm(up_s[block(k), :], u_t[...], NN)

    wide = [functools.partial(add_wide, dwd, grad_b, hid_s, TT, h) for h in range(2)]
    backs = tri_pieces(tri, hid_s, wide[:1], (wide[1], lambda: add_small_nt(small_u, u_b)))
    staged(dot, gelu_act(pre_out, new_s), backs, ((hid_s, new_s),), (tri, small_u, dwd), setup)


def stage3(pre_in, grad, w_down, w_up, u_b, err_out, tri, dwu, new_s, g_s):
    def dot(k):
        return mm(w_down[0, block(k), :], grad[...], NT)

    def act(k, value):
        d_hid = value.astype(bf16).astype(f32)
        pre = pre_in[block(k), :].astype(f32)
        sig, cubic = half_sig(pre)
        new_s[block(k), :] = (d_hid * gelu_back(pre, sig, cubic)[1]).astype(bf16)

    def up():
        err_out[...] = mm(w_up[0], g_s[...], NN).astype(bf16)

    wide = [functools.partial(add_wide, dwu, u_b, g_s, NT, h) for h in range(2)]
    staged(dot, act, tri_pieces(tri, g_s, wide, (up,)), ((g_s, new_s),), (tri, dwu))


def stage4(pre_in, err_t, w_down, tok_b, err_b, g_out, small_q, dwd, dwu, new_h, hid_s, new_g, g_s):
    def dot(k):
        return mm(w_down[0, block(k), :], err_t[...], NN)

    def act(k, value):
        d_hid = value.astype(bf16).astype(f32)
        pre = pre_in[block(k), :].astype(f32)
        sig, cubic = half_sig(pre)
        hid, slope = gelu_back(pre, sig, cubic)
        new_h[block(k), :] = hid.astype(bf16)
        grad_up = (d_hid * slope).astype(bf16)
        new_g[block(k), :] = grad_up
        g_out[block(k), :] = grad_up

    def part(q, h):
        if q:
            dwd[h, :, :] += mm(err_b[...], hid_s[h * FF // 2:(h + 1) * FF // 2, :], NT)
        else:
            dwu[h, :, :] += mm(tok_b[...], g_s[h * FF // 2:(h + 1) * FF // 2, :], TT)

    backs = [functools.partial(part, q, h) for q in range(2) for h in range(2)]
    backs += [lambda: add_small_nt(small_q, err_b), lambda: None]
    staged(dot, act, backs, ((hid_s, new_h), (g_s, new_g)), (small_q, dwd, dwu))


def stage5(g_in, tri):
    zero_first((tri,))
    add_tri(tri, g_in)


SMALL = (2, 128, 384)
WIDE = (2, 384, 768)
TRI_SHAPE = (2, TRI // 2, B)
FORMS = {
    "tri": (TRI_SHAPE, ((512, ORDER_Y), (384, ORDER_X), (512, ORDER_X), (384, ORDER_Z), (384, ORDER_X), (512, ORDER_Y))),
    "wide": (WIDE, ((128, ORDER_Z), (128, ORDER_X), (128, ORDER_Y))),
    "small": (SMALL, ((128, ORDER_Y),)),
}


def flows_of(name, form):
    shape, cuts = FORMS[form]
    flows, row = [], 0
    for rows, order in cuts:
        flows.append(Flow(name, row, rows, shape[2], order, row // 16, form == "wide"))
        row += rows
    return flows


def precise(left, right):
    return lax.dot_general(left, right, NN, precision=lax.Precision.HIGHEST, preferred_element_type=f32)


def thirds(x):
    parts = []
    for _ in range(3):
        parts.append(x.astype(bf16))
        x = x - parts[-1].astype(f32)
    return parts


def tile_spec(kind, shape, tile):
    n = shape[0 if kind[0] == "r" else 1] // tile

    def at(i):
        if "b" in kind:
            return jnp.maximum(i - 1, 0)
        return jnp.minimum(i, n - 1) if "f" in kind else i

    if kind[0] == "r":
        return pl.BlockSpec((tile, D), lambda i: (at(i), 0))
    return pl.BlockSpec((shape[0], tile), lambda i: (0, at(i)))


def whole_spec(shape):
    zeros = (0,) * len(shape)
    return pl.BlockSpec(shape, lambda i: zeros, pipeline_mode=pl.Buffered(1))


def block_spec(shape, b):
    return pl.BlockSpec((1,) + shape[1:], lambda i: (b, 0, 0), pipeline_mode=pl.Buffered(1))


ANY = pl.BlockSpec(memory_space=pl.ANY)


class Board:
    def __init__(self):
        self.flows, self.firsts, self.arrays, self.forms, self.fresh = [], [], {}, {}, 0

    def add(self, name, form, array, inverse=None, block=0):
        flows = flows_of(name, form)
        self.flows += flows
        self.forms[name] = FORMS[form][0]
        self.arrays[name + ":src"] = array.reshape(self.forms[name])
        if inverse is not None:
            self.firsts.append(First(name, flows, inverse, block))
            self.arrays[name + ":inv"] = inverse

    def plan(self, tick_us, last):
        for f in self.flows:
            f.at = f.b if hasattr(f, "b") else f.at
        flows = [f for f in self.flows if f.at < LAST and not (f.wide and f.at == 5)]
        idle = [f for f in self.flows if f.wide and f.at == 5]
        for f in idle:
            f.a = f.b = f.at
        slots, rest, end = plan(flows, self.firsts, tick_us, last)
        runs = [f for f in self.firsts if f.fans[0] in flows]
        self.firsts = [f for f in self.firsts if f not in runs]
        self.flows = [f for f in flows + idle if f.b < LAST or f.a < f.b]
        moving = [f for f in flows if f.a < f.b]
        ins, outs = [], {}
        for f in moving:
            if f.a == 0:
                ins.append(f.name + ":src")
            elif f.a < 5 or (f.a == 5 and not f.wide):
                ins.append(f.part + ":in")
            if f.b <= 5:
                outs[f.part + ":out"] = (f.kept(f.b), f.cols)
            else:
                outs[f.name + ":dst"] = self.forms[f.name]
        for first in runs:
            ins.append(first.name + ":inv")
            ins += [f.part + ":in" for f in first.flows if f.part + ":out" not in outs]
        ins += [name for name in outs if name in self.arrays]
        return slots, rest, end, moving, runs, list(dict.fromkeys(ins)), outs

    def keep(self, outs, values):
        for name, value in zip(outs, values):
            self.arrays[name.replace(":out", ":in")] = value


def run_stage(board, body, name, tile, tick_us, ins, outs, scratch, flops, cid, last=False):
    def spec(kind, shape):
        if kind == "w":
            return whole_spec(shape)
        return block_spec(shape, kind) if isinstance(kind, int) else tile_spec(kind, shape, tile)

    steps = len(tick_us)
    slots, rest, end, moving, runs, m_ins, m_outs = board.plan(tick_us, last)
    scr = [job.open(job.a, job.b) if isinstance(job, Flow) else job.open() for job in runs + moving]
    n_in, n_min, n_out, n_mout, n_scr = len(ins), len(m_ins), len(outs), len(m_outs), len(scratch)

    def kernel(*refs):
        refs = list(refs)

        def pull(n):
            return [refs.pop(0) for _ in range(n)]

        c_in, m_in, c_out, m_out, c_scr = pull(n_in), pull(n_min), pull(n_out), pull(n_mout), pull(n_scr)
        named = dict(zip(m_ins, m_in))
        named.update(zip(m_outs, m_out))
        step = pl.program_id(0)
        events = {}
        if moving:
            pl.when(step == 0)(entry_barrier)
        for job, s in zip(runs + moving, scr):
            events[job] = job.bind(named, pull(len(s)))

        def fire(slot):
            for job, what, s in slot:
                if what in ("go", "stop"):
                    events[job][what](s)
                else:
                    events[job][what]()

        for t in range(steps):
            if slots[t]:
                pl.when(step == t)(functools.partial(fire, slots[t]))
        if body is not None:
            body(*c_in, *c_out, *c_scr)
        if rest:
            pl.when(step == steps - 1)(functools.partial(fire, rest))

    params = dict(vmem_limit_bytes=63 * MIB)
    if moving:
        params.update(collective_id=cid, has_side_effects=True)
    values = pl.pallas_call(
        kernel, grid=(steps,),
        in_specs=[spec(kind, arr.shape) for arr, kind in ins] + [ANY] * n_min,
        out_specs=[spec(kind, shape) for shape, dtype, kind in outs] + [ANY] * n_mout,
        out_shape=[jax.ShapeDtypeStruct(shape, dtype) for shape, dtype, kind in outs]
        + [jax.ShapeDtypeStruct(shape, f32) for shape in m_outs.values()],
        scratch_shapes=list(scratch) + [x for s in scr for x in s],
        input_output_aliases={n_in + m_ins.index(m): n_out + i for i, m in enumerate(m_outs) if m in m_ins},
        compiler_params=pltpu.CompilerParams(**params),
        cost_estimate=pl.CostEstimate(flops=flops, bytes_accessed=40 * MIB, transcendentals=0),
        name=name)(*[arr for arr, _ in ins], *[board.arrays[m] for m in m_ins])
    board.keep(m_outs, values[n_out:])
    return values[:n_out]


def final_kernel(decay, t0, t1, t2, t3, n0, n1, n2, n3, old_s, old_a, s0, s1, s2, s3, old_u, old_q, inv_u, inv_q,
                 new_s, new_a, p_up, p_down, new_u, new_q, pk, od, nw, tr, nv, pv, pt, inv_s, sem_in, sem_out):
    rho = decay[0]
    scale = (1.0 - rho) * decay[1]
    deep = pk.shape[0]
    units = []
    for q, (src, old, new) in enumerate(((t0, old_a, new_a), (t1, old_a, new_a), (t2, old_s, new_s), (t3, old_s, new_s))):
        n = (n0, n1, n2, n3)[q]
        off = 0
        for j in range(NB):
            units.append((q, src, old, new, q % 2, j, off, n))
            off += (j + 1) * B

    def loads(u):
        q, src, old, new, b, j, off, n = units[u]
        rows, s = (j + 1) * B, u % deep
        parts = ((src.at[pl.ds(off, rows), :], pk.at[s, pl.ds(0, rows), :]),
                 (old.at[b, pl.ds(0, rows), pl.ds(j * B, B)], od.at[s, pl.ds(0, rows), :]),
                 (n.at[j // 3, :, pl.ds(j % 3 * B, B)], nv.at[s]))
        return [pltpu.make_async_copy(x, y, sem_in.at[s, i]) for i, (x, y) in enumerate(parts)]

    def stores(u):
        q, src, old, new, b, j, off, n = units[u]
        rows, s = (j + 1) * B, u % deep
        parts = [(nw.at[s, pl.ds(0, rows), :], new.at[b, pl.ds(0, rows), pl.ds(j * B, B)])]
        if q < 2:
            parts.append((pv.at[s], p_up.at[b, :, pl.ds(j * B, B)]))
        else:
            parts.append((pt.at[s], p_down.at[b, pl.ds(j * B, B), :]))
        if j:
            parts.append((tr.at[s, :, pl.ds(0, j * B)], new.at[b, pl.ds(j * B, B), pl.ds(0, j * B)]))
        return [pltpu.make_async_copy(x, y, sem_out.at[s, i]) for i, (x, y) in enumerate(parts)]

    for u in range(deep - 1):
        for c in loads(u):
            c.start()
    h = 128
    for acc, old, new, b in ((s0, old_u, new_u, 0), (s1, old_u, new_u, 1), (s2, old_q, new_q, 0), (s3, old_q, new_q, 1)):
        top = rho * old[b, :h, :] + scale * acc[0]
        mid = rho * old[b, h:B, h:] + scale * acc[1, :, :B]
        low = rho * old[b, B:, B:] + scale * acc[1, :, B:]
        new[b, :h, :] = top
        new[b, h:B, h:] = mid
        new[b, B:, B:] = low
        new[b, h:, :h] = top[:, h:].T
        new[b, B:, h:B] = mid[:, h:].T
    for u, (q, src, old, new, b, j, off, n) in enumerate(units):
        s = u % deep
        for c in loads(u):
            c.wait()
        if u >= deep:
            for c in stores(u - deep):
                c.wait()
        for i in range(j + 1):
            here = slice(i * B, (i + 1) * B)
            part = rho * od[s, here, :] + scale * pk[s, here, :]
            nw[s, here, :] = part
            if i < j:
                tr[s, :, here] = part.T
        if j == 0:
            x, y, z = thirds((inv_u if q < 2 else inv_q)[b])
            for i, third in enumerate((x, x, y, x, y, z)):
                inv_s[:, i * D:(i + 1) * D] = third
        x, y, z = thirds(nv[s])
        prod = mm(inv_s[...], jnp.concatenate((x, y, x, z, y, x), axis=0), NN) * decay[1]
        if q < 2:
            pv[s] = prod
        else:
            pt[s] = prod.T
        for c in stores(u):
            c.start()
        if u + deep - 1 < len(units):
            for c in loads(u + deep - 1):
                c.start()
    for u in range(len(units) - deep, len(units)):
        for c in stores(u):
            c.wait()


def finish(decay, tris, smalls, prods, s_up_old, a_down_old, a_up_old, s_down_old, inv_u, inv_q):
    vmem = pl.BlockSpec(memory_space=pltpu.VMEM)
    big = jax.ShapeDtypeStruct(s_up_old.shape, f32)
    small = jax.ShapeDtypeStruct(a_up_old.shape, f32)
    deep = 4
    return pl.pallas_call(
        final_kernel,
        in_specs=[pl.BlockSpec(memory_space=pltpu.SMEM)] + [ANY] * 10 + [vmem] * 8,
        out_specs=[ANY] * 4 + [vmem] * 2,
        out_shape=[big, big, jax.ShapeDtypeStruct((2, D, FF), f32), jax.ShapeDtypeStruct((2, FF, D), f32), small, small],
        scratch_shapes=[pltpu.VMEM((deep, FF, B), f32)] * 3 + [pltpu.VMEM((deep, B, FF), f32)]
        + [pltpu.VMEM((deep, D, B), f32)] * 2 + [pltpu.VMEM((deep, B, D), f32), pltpu.VMEM((D, 6 * D), bf16)] + [pltpu.SemaphoreType.DMA((deep, 3))] * 2,
        compiler_params=pltpu.CompilerParams(vmem_limit_bytes=63 * MIB),
        name="finish")(decay, *[t.reshape(TRI, B) for t in tris], *prods, s_up_old, a_down_old, *smalls,
                       a_up_old, s_down_old, inv_u, inv_q)


def solution(mesh):
    axis_size = mesh.shape["data"]
    tile = 512

    def local_step(tok, grad, w_up, w_down, a_up_old, s_up_old, a_down_old, s_down_old,
                   a_up_inv, s_up_inv, a_down_inv, s_down_inv, factor_decay):
        total = tok.shape[0]
        steps = total // tile
        inv_n = 1.0 / (total * axis_size)
        acts = [pltpu.VMEM((FF, tile), bf16)] * 2
        w_t = pltpu.VMEM((FF, D), bf16)
        unit = 2 * total * FF * D
        wide_out, small_out, tri_out = (WIDE, f32, "w"), (SMALL, f32, "w"), ((TRI, B), f32, "w")
        long_out, short_out = ((FF, total), bf16, "cf"), ((D, total), bf16, "cb")
        board = Board()
        pre0, u1, ad0, au0, sd1 = run_stage(
            board, stage1, "stage1", tile, [0.0] * (steps + 1),
            ((tok, "rf"), (grad, "rf"), (w_up, 0), (w_down, 0), (tok, "rb"), (grad, "rb")),
            (long_out, short_out, tri_out, small_out, small_out), acts + [w_t, pltpu.VMEM((D, FF), bf16)], 5 * unit, 0)
        board.add("ad0", "tri", ad0)
        board.add("au0", "small", au0)
        board.add("sd1", "small", sd1)
        pre1, ad1, au1, dwd1 = run_stage(
            board, stage2, "stage2", tile, [2.0] + [3.5] * steps, ((u1, "cf"), (w_up, 1), (u1, "cb"), (grad, "rb")),
            (long_out, tri_out, small_out, wide_out), acts + [w_t], 5 * unit, 1)
        board.add("ad1", "tri", ad1)
        board.add("au1", "small", au1)
        board.add("dwd1", "wide", dwd1, a_down_inv, 1)
        e1, su1, dwu1 = run_stage(
            board, stage3, "stage3", tile, [2.0] + [4.1] * steps,
            ((pre1, "cf"), (grad, "rf"), (w_down, 1), (w_up, 1), (u1, "cb")), (short_out, tri_out, wide_out), acts, 6 * unit, 2)
        board.add("su1", "tri", su1)
        board.add("dwu1", "wide", dwu1, s_up_inv, 1)
        g0, sd0, dwd0, dwu0 = run_stage(
            board, stage4, "stage4", tile, [2.0] + [3.1] * steps,
            ((pre0, "cf"), (e1, "cf"), (w_down, 0), (tok, "rb"), (e1, "cb")),
            (long_out, small_out, wide_out, wide_out), acts * 2, 4 * unit, 3)
        board.add("sd0", "small", sd0)
        board.add("dwd0", "wide", dwd0, a_down_inv, 0)
        board.add("dwu0", "wide", dwu0, s_up_inv, 0)
        su0, = run_stage(board, stage5, "stage5", tile, [1.9] * steps, ((g0, "c"),), (tri_out,), [], 3 * unit, 4)
        board.add("su0", "tri", su0)
        run_stage(board, None, "tail", tile, [0.1], (), (), [], unit, 5, last=True)
        done = board.arrays
        decay = jnp.stack((factor_decay, jnp.float32(inv_n)))
        new_s, new_a, p_up, p_down, new_u, new_q = finish(
            decay, [done[n + ":dst"] for n in ("ad0", "ad1", "su0", "su1")],
            [done[n + ":dst"] for n in ("au0", "au1", "sd0", "sd1")],
            [done[n + ":dst"] for n in ("dwu0", "dwu1", "dwd0", "dwd1")],
            s_up_old, a_down_old, a_up_old, s_down_old, a_up_inv, s_down_inv)
        return p_up, p_down, new_u, new_s, new_a, new_q

    batch_spec = P("data", None)
    replicated = P()
    return jax.shard_map(local_step, mesh=mesh, in_specs=(batch_spec, batch_spec) + (replicated,) * 11,
                         out_specs=(replicated,) * 6, check_vma=False)
```

profile of v0, /device:TPU:0, one launch (start us, length us, event | category | flops | bytes accessed | tf_op | source)
XLA Modules:
  0.0 469.5 jit_solution(2013858147954970975)
XLA Ops:
  0.6 63.6 %stage1.1 = (bf16[1536,8192]{1,0:T(8,128)(2,1)}, bf16[384,8192]{1,0:T(8,128)(2,1)}, f32[5376,256]{1,0:T(8,128)}, f32[2,128,384]{2,1,0:T(8,128)}, f32[2,128,384]{2,1,0:T(8,128)}) custom-call(bf16[8192,384]{1,0:T(8,128)(2,1)} %refs_3_.7, bf16[8192,384]{1,0:T(8,128)(2,1)} %refs_1_.5, bf16[2,384,1536]{2,1,0:T(8,128)(2,1)} %refs_3_.6, ...), custom_call_target="tpu_custom_call" | custom-call | flops 48318382080 | bytes 41943040 | tf_op jit(solution)/shard_map/stage1/pallas_call | solution.py:692
  64.3 74.3 %stage2.1 = (bf16[1536,8192]{1,0:T(8,128)(2,1)}, f32[5376,256]{1,0:T(8,128)}, f32[2,128,384]{2,1,0:T(8,128)}, f32[2,384,768]{2,1,0:T(8,128)}, f32[2,2688,256]{2,...) custom-call(bf16[384,8192]{1,0:T(8,128)(2,1)} %get-tuple-element.66.refs_0_.refs_2_.refs_4_, ...), custom_call_target="tpu_custom_call" | custom-call | flops 48318382080 | bytes 41943040 | tf_op jit(solution)/shard_map/stage2/pallas_call | solution.py:692
  138.6 85.5 %stage3.1 = (bf16[384,8192]{1,0:T(8,128)(2,1)}, f32[5376,256]{1,0:T(8,128)}, f32[2,384,768]{2,1,0:T(8,128)}, f32[2,2688,256]{2,1,0:T(8,128)}, f32[2,128,384]{2,1...) custom-call(bf16[1536,8192]{1,0:T(8,128)(2,1)} %get-tuple-element.70, ...), custom_call_target="tpu_custom_call", output_to_operand_aliasing={{3}: (8, {}), {4}: (9, {}), {5}: (10, {})} | custom-call | flops 57982058496 | bytes 41943040 | tf_op jit(solution)/shard_map/stage3/pallas_call | solution.py:692
  224.0 71.8 %stage4.1 = (bf16[1536,8192]{1,0:T(8,128)(2,1)}, f32[2,128,384]{2,1,0:T(8,128)}, f32[2,384,768]{2,1,0:T(8,128)}, f32[2,384,768]{2,1,0:T(8,128)}, f32[2,2688,256]...) custom-call(bf16[1536,8192]{1,0:T(8,128)(2,1)} %get-tuple-element.78, ...), custom_call_target="tpu_custom_call", output_to_operand_aliasing={{4}: (11, {}), {5}: (12, {})} | custom-call | flops 38654705664 | bytes 41943040 | tf_op jit(solution)/shard_map/stage4/pallas_call | solution.py:692
  295.8 43.2 %stage5.1 = (f32[5376,256]{1,0:T(8,128)}, f32[2,2688,256]{2,1,0:T(8,128)}, f32[2,128,384]{2,1,0:T(8,128)}, f32[2,2688,256]{2,1,0:T(8,128)}, f32[2,384,768]{2,1,0...) custom-call(bf16[1536,8192]{1,0:T(8,128)(2,1)} %get-tuple-element.87, ...), custom_call_target="tpu_custom_call", output_to_operand_aliasing={{1}: (8, {}), {2}: (9, {}), {3}: (10, {}), {4}: (11, {})} | custom-call | flops 28991029248 | bytes 41943040 | tf_op jit(solution)/shard_map/stage5/pallas_call | solution.py:692
  339.0 86.8 %tail.1 = (f32[2,2688,256]{2,1,0:T(8,128)}, f32[2,384,768]{2,1,0:T(8,128)}, f32[2,128,384]{2,1,0:T(8,128)}, f32[8,768]{1,0:T(8,128)}, f32[8,768]{1,0:T(8,128)}, ...) custom-call(f32[8,384]{1,0:T(8,128)} %get-tuple-element.99.refs_0_, ...), custom_call_target="tpu_custom_call", output_to_operand_aliasing={{0}: (10, {}), {1}: (11, {}), {8}: (12, {})} | custom-call | flops 9663676416 | bytes 41943040 | tf_op jit(solution)/shard_map/tail/pallas_call | solution.py:692
  426.5 0.6 pad_maximum_fusion.decay
  427.1 42.1 %finish.1 = (f32[2,1536,1536]{2,1,0:T(8,128)}, f32[2,1536,1536]{2,1,0:T(8,128)}, f32[2,384,1536]{2,1,0:T(8,128)}, f32[2,1536,384]{2,1,0:T(8,128)}, f32[2,384,384]{2,1,0:T(8,128)}, /*index=5*/f32[2,384,384]{2,1,0:T(8,128)}) custom-call(f32[2]{0:T(128)} %pad_maximum_fusion.decay, f32[5376,256]{1,0:T(8,128)} %bitcast.14, f32[5376,256]{1,0:T(8,128)} %bitcast.13, ...), custom_call_target="tpu_custom_call" | custom-call | tf_op jit(solution)/shard_map/finish/pallas_call | solution.py:791
where the time goes:
time: 475 us; the launch traced here: 470 us
  Pallas kernels  467 us (98%)
    pallas_call x6, Pallas kernels, run_stage(): pl.pallas_call(kernel, grid=(steps,), in_specs=[spec(kind, arr.shape) for...  425 us
    pallas_call x1, Pallas kernels, finish(): pl.pallas_call(final_kernel, in_specs=[pl.BlockSpec(memory_space=pltpu.SM...  42.1 us

commit v1 on v0

--- a/solution.py
+++ b/solution.py
@@ -63,7 +63,8 @@
 
 
 MESH = pl.DeviceIdType.MESH
-ORDER_X, ORDER_Y, ORDER_Z = (1, 2, 3, 4), (2, 1, 3, 4), (3, 4, 1, 2)
+ORDER_X, ORDER_Y, ORDER_Z, ORDER_A, ORDER_B = (
+    tuple(map(int, order)) for order in ("1234", "2134", "3412", "1342", "2341"))
 LINKS = {0: {0: 6e5}, 1: {1: 45e3}, 2: {2: 45e3}, 3: {3: 45e3}, 4: {3: 45e3, 4: 23e3}}
 LAG = 2.5
 SLACK = 3.0
@@ -97,7 +98,7 @@
 class Flow:
     def __init__(self, name, row0, rows, cols, order, shard_row, wide):
         self.name, self.row0, self.rows, self.cols, self.order = name, row0, rows, cols, order
-        self.shard_row, self.wide = shard_row, wide
+        self.shard_row, self.wide, self.old = shard_row, wide, None
         self.at, self.start = 0, 0.0
         self.part = name + ":part%d" % row0
 
@@ -120,13 +121,18 @@
     def open(self, a, b):
         self.a, self.b = a, b
         n = b - a
-        out = [pltpu.SemaphoreType.DMA((2,)), pltpu.SemaphoreType.DMA((n,)), pltpu.SemaphoreType.DMA((n,))]
+        out = [pltpu.SemaphoreType.DMA((3,)), pltpu.SemaphoreType.DMA((n,)), pltpu.SemaphoreType.DMA((n,))]
         if a < 5:
             out.append(pltpu.VMEM((self.rows if a == 0 else self.kept(a), self.cols), f32))
             out.append(pltpu.VMEM((sum(self.length(s) for s in range(a, min(b, 5))), self.cols), f32))
+            if self.mixes():
+                out.append(pltpu.VMEM((self.kept(5), self.cols), f32))
         elif a == 5 and not self.wide:
             out.append(pltpu.VMEM((self.kept(5), self.cols), f32))
         return out
+
+    def mixes(self):
+        return self.old is not None and self.a < 5 <= self.b
 
     def bind(self, named, scr):
         a, b, row0, rows = self.a, self.b, self.row0, self.rows
@@ -142,7 +148,7 @@
         base = offs[min(max(a, 1), 5) - 1]
         work = recv = None
         if a < 5:
-            work, recv = scr[3:]
+            work, recv = scr[3:5]
         elif a == 5:
             work = named[self.name + ":first"].at[pl.ds(self.shard_row, 8), :] if self.wide else scr[3]
         sends, begin_recv, locals_ = {}, {}, []
@@ -171,7 +177,14 @@
             else:
                 k = LAST - 1 - s
                 sends[s] = remote(s, final() if s == 5 else spot(k), spot(k))
-        load = place = save = None
+        load = place = save = old = None
+        if self.mixes():
+            old_array, half = self.old
+            spot4 = core * half + row0 + offs[4]
+            j = sum((spot4 // (B // 2 * m * (m + 1)) + 31) // 32 for m in range(1, NB))
+            old = pltpu.make_async_copy(
+                named[self.name + ":old"].at[old_array, pl.ds(al(spot4 - B // 2 * j * (j + 1)), lens[4]),
+                                             pl.ds(pl.multiple_of(j * B, B), B)], scr[5], sem_l.at[2])
         if a == 0:
             load = pltpu.make_async_copy(src.at[core, pl.ds(row0, rows), :], work, sem_l.at[0])
         elif a < 5 or (a == 5 and not self.wide):
@@ -188,6 +201,12 @@
                 x, y = al(row + q), al(frm + q)
                 work[pl.ds(x, step), :] = work[pl.ds(x, step), :] + recv[pl.ds(y, step), :]
 
+        def mix():
+            rho = named["decay"][0]
+            x, y = pl.ds(al(offs[4] - base), lens[4]), pl.ds(begin_recv[4], lens[4])
+            total = (work[x, :] + recv[y, :]) * named["decay"][1]
+            work[x, :] = rho * scr[5][...] + (1.0 - rho) * total
+
         def take(s, then):
             if s == a and load is not None and a == 0:
                 load.wait()
@@ -195,6 +214,10 @@
             if s == 5 and place is not None:
                 place.wait()
             if s >= 5:
+                then()
+            elif s == 4 and old is not None:
+                old.wait()
+                mix()
                 then()
             elif s == 4 or s + 1 == b:
                 add(offs[s] - base, begin_recv[s], lens[s])
@@ -213,6 +236,8 @@
 
         def begin():
             load.start()
+            if old is not None:
+                old.start()
             if a == 0:
                 send(0)
 
@@ -439,6 +464,19 @@
             back()
 
 
+def plain(dot, act, backs, accs, setup):
+    @pl.when(pl.program_id(0) == 0)
+    def _():
+        for acc in accs:
+            acc[...] = jnp.zeros_like(acc)
+        setup()
+
+    for k in range(NB):
+        act(k, dot(k))
+    for back in backs:
+        back()
+
+
 def block(k):
     return slice(k * B, (k + 1) * B)
 
@@ -464,7 +502,7 @@
     return act
 
 
-def stage1(tok, grad, w_up, w_down, tok_b, grad_b, pre_out, next_out, tri, small_u, small_q, new_s, hid_s, up_s, down_s):
+def stage1(tok, grad, w_up, w_down, pre_out, next_out, tri, small_u, small_q, hid_s, up_s, down_s):
     def setup():
         up_s[...] = w_up[0].T
         down_s[...] = w_down[0].T
@@ -475,8 +513,12 @@
     def down():
         next_out[...] = mm(down_s[...], hid_s[...], NN).astype(bf16)
 
-    backs = tri_pieces(tri, hid_s, (down,), (lambda: add_small_tn(small_u, tok_b), lambda: add_small_tn(small_q, grad_b)))
-    staged(dot, gelu_act(pre_out, new_s), backs, ((hid_s, new_s),), (tri, small_u, small_q), setup)
+    def smalls():
+        add_small_tn(small_u, tok)
+        add_small_tn(small_q, grad)
+
+    backs = [functools.partial(tri_col, tri, hid_s, j) for j in range(NB)] + [down, smalls]
+    plain(dot, gelu_act(pre_out, hid_s), backs, (tri, small_u, small_q), setup)
 
 
 def add_wide(acc, left, mat, dims, h):
@@ -546,9 +588,9 @@
 WIDE = (2, 384, 768)
 TRI_SHAPE = (2, TRI // 2, B)
 FORMS = {
-    "tri": (TRI_SHAPE, ((512, ORDER_Y), (384, ORDER_X), (512, ORDER_X), (384, ORDER_Z), (384, ORDER_X), (512, ORDER_Y))),
-    "wide": (WIDE, ((128, ORDER_Z), (128, ORDER_X), (128, ORDER_Y))),
-    "small": (SMALL, ((128, ORDER_Y),)),
+    "tri": (TRI_SHAPE, ((512, ORDER_X), (512, ORDER_B), (512, ORDER_X), (512, ORDER_Z), (512, ORDER_Y), (128, ORDER_B))),
+    "wide": (WIDE, ((128, ORDER_Y), (128, ORDER_Y), (128, ORDER_A))),
+    "small": (SMALL, ((128, ORDER_X),)),
 }
 
 
@@ -596,20 +638,25 @@
 
 
 ANY = pl.BlockSpec(memory_space=pl.ANY)
+SCALARS = pl.BlockSpec(memory_space=pltpu.SMEM)
 
 
 class Board:
     def __init__(self):
         self.flows, self.firsts, self.arrays, self.forms, self.fresh = [], [], {}, {}, 0
 
-    def add(self, name, form, array, inverse=None, block=0):
+    def add(self, name, form, array, other=None, block=0):
         flows = flows_of(name, form)
         self.flows += flows
         self.forms[name] = FORMS[form][0]
         self.arrays[name + ":src"] = array.reshape(self.forms[name])
-        if inverse is not None:
-            self.firsts.append(First(name, flows, inverse, block))
-            self.arrays[name + ":inv"] = inverse
+        if form == "wide":
+            self.firsts.append(First(name, flows, other, block))
+            self.arrays[name + ":inv"] = other
+        elif form == "tri":
+            for f in flows:
+                f.old = (block, TRI // 2)
+            self.arrays[name + ":old"] = other
 
     def plan(self, tick_us, last):
         for f in self.flows:
@@ -629,6 +676,8 @@
                 ins.append(f.name + ":src")
             elif f.a < 5 or (f.a == 5 and not f.wide):
                 ins.append(f.part + ":in")
+            if f.mixes():
+                ins += ["decay", f.name + ":old"]
             if f.b <= 5:
                 outs[f.part + ":out"] = (f.kept(f.b), f.cols)
             else:
@@ -691,7 +740,7 @@
         params.update(collective_id=cid, has_side_effects=True)
     values = pl.pallas_call(
         kernel, grid=(steps,),
-        in_specs=[spec(kind, arr.shape) for arr, kind in ins] + [ANY] * n_min,
+        in_specs=[spec(kind, arr.shape) for arr, kind in ins] + [SCALARS if m == "decay" else ANY for m in m_ins],
         out_specs=[spec(kind, shape) for shape, dtype, kind in outs] + [ANY] * n_mout,
         out_shape=[jax.ShapeDtypeStruct(shape, dtype) for shape, dtype, kind in outs]
         + [jax.ShapeDtypeStruct(shape, f32) for shape in m_outs.values()],
@@ -704,31 +753,30 @@
     return values[:n_out]
 
 
-def final_kernel(decay, t0, t1, t2, t3, n0, n1, n2, n3, old_s, old_a, s0, s1, s2, s3, old_u, old_q, inv_u, inv_q,
-                 new_s, new_a, p_up, p_down, new_u, new_q, pk, od, nw, tr, nv, pv, pt, inv_s, sem_in, sem_out):
+def final_kernel(decay, t0, t1, t2, t3, n0, n1, n2, n3, s0, s1, s2, s3, old_u, old_q, inv_u, inv_q,
+                 new_s, new_a, p_up, p_down, new_u, new_q, pk, tr, nv, pv, pt, inv_s, sem_in, sem_out):
     rho = decay[0]
     scale = (1.0 - rho) * decay[1]
     deep = pk.shape[0]
+    ahead = deep // 2
     units = []
-    for q, (src, old, new) in enumerate(((t0, old_a, new_a), (t1, old_a, new_a), (t2, old_s, new_s), (t3, old_s, new_s))):
-        n = (n0, n1, n2, n3)[q]
+    for q, (src, new, n) in enumerate(((t0, new_a, n0), (t1, new_a, n1), (t2, new_s, n2), (t3, new_s, n3))):
         off = 0
         for j in range(NB):
-            units.append((q, src, old, new, q % 2, j, off, n))
+            units.append((q, src, new, q % 2, j, off, n))
             off += (j + 1) * B
 
     def loads(u):
-        q, src, old, new, b, j, off, n = units[u]
+        q, src, new, b, j, off, n = units[u]
         rows, s = (j + 1) * B, u % deep
         parts = ((src.at[pl.ds(off, rows), :], pk.at[s, pl.ds(0, rows), :]),
-                 (old.at[b, pl.ds(0, rows), pl.ds(j * B, B)], od.at[s, pl.ds(0, rows), :]),
                  (n.at[j // 3, :, pl.ds(j % 3 * B, B)], nv.at[s]))
         return [pltpu.make_async_copy(x, y, sem_in.at[s, i]) for i, (x, y) in enumerate(parts)]
 
     def stores(u):
-        q, src, old, new, b, j, off, n = units[u]
+        q, src, new, b, j, off, n = units[u]
         rows, s = (j + 1) * B, u % deep
-        parts = [(nw.at[s, pl.ds(0, rows), :], new.at[b, pl.ds(0, rows), pl.ds(j * B, B)])]
+        parts = [(pk.at[s, pl.ds(0, rows), :], new.at[b, pl.ds(0, rows), pl.ds(j * B, B)])]
         if q < 2:
             parts.append((pv.at[s], p_up.at[b, :, pl.ds(j * B, B)]))
         else:
@@ -737,10 +785,10 @@
             parts.append((tr.at[s, :, pl.ds(0, j * B)], new.at[b, pl.ds(j * B, B), pl.ds(0, j * B)]))
         return [pltpu.make_async_copy(x, y, sem_out.at[s, i]) for i, (x, y) in enumerate(parts)]
 
-    for u in range(deep - 1):
+    for u in range(ahead):
         for c in loads(u):
             c.start()
-    h = 128
+    h = B // 2
     for acc, old, new, b in ((s0, old_u, new_u, 0), (s1, old_u, new_u, 1), (s2, old_q, new_q, 0), (s3, old_q, new_q, 1)):
         top = rho * old[b, :h, :] + scale * acc[0]
         mid = rho * old[b, h:B, h:] + scale * acc[1, :, :B]
@@ -750,19 +798,13 @@
         new[b, B:, B:] = low
         new[b, h:, :h] = top[:, h:].T
         new[b, B:, h:B] = mid[:, h:].T
-    for u, (q, src, old, new, b, j, off, n) in enumerate(units):
+    for u, (q, src, new, b, j, off, n) in enumerate(units):
         s = u % deep
         for c in loads(u):
             c.wait()
-        if u >= deep:
-            for c in stores(u - deep):
-                c.wait()
-        for i in range(j + 1):
+        for i in range(j):
             here = slice(i * B, (i + 1) * B)
-            part = rho * od[s, here, :] + scale * pk[s, here, :]
-            nw[s, here, :] = part
-            if i < j:
-                tr[s, :, here] = part.T
+            tr[s, :, here] = pk[s, here, :].T
         if j == 0:
             x, y, z = thirds((inv_u if q < 2 else inv_q)[b])
             for i, third in enumerate((x, x, y, x, y, z)):
@@ -775,29 +817,32 @@
             pt[s] = prod.T
         for c in stores(u):
             c.start()
-        if u + deep - 1 < len(units):
-            for c in loads(u + deep - 1):
+        if u + ahead < len(units):
+            if u + ahead >= deep:
+                for c in stores(u + ahead - deep):
+                    c.wait()
+            for c in loads(u + ahead):
                 c.start()
     for u in range(len(units) - deep, len(units)):
         for c in stores(u):
             c.wait()
 
 
-def finish(decay, tris, smalls, prods, s_up_old, a_down_old, a_up_old, s_down_old, inv_u, inv_q):
+def finish(decay, tris, smalls, prods, s_up_old, a_up_old, s_down_old, inv_u, inv_q):
     vmem = pl.BlockSpec(memory_space=pltpu.VMEM)
     big = jax.ShapeDtypeStruct(s_up_old.shape, f32)
     small = jax.ShapeDtypeStruct(a_up_old.shape, f32)
-    deep = 4
+    deep = 6
     return pl.pallas_call(
         final_kernel,
-        in_specs=[pl.BlockSpec(memory_space=pltpu.SMEM)] + [ANY] * 10 + [vmem] * 8,
+        in_specs=[SCALARS] + [ANY] * 8 + [vmem] * 8,
         out_specs=[ANY] * 4 + [vmem] * 2,
         out_shape=[big, big, jax.ShapeDtypeStruct((2, D, FF), f32), jax.ShapeDtypeStruct((2, FF, D), f32), small, small],
-        scratch_shapes=[pltpu.VMEM((deep, FF, B), f32)] * 3 + [pltpu.VMEM((deep, B, FF), f32)]
-        + [pltpu.VMEM((deep, D, B), f32)] * 2 + [pltpu.VMEM((deep, B, D), f32), pltpu.VMEM((D, 6 * D), bf16)] + [pltpu.SemaphoreType.DMA((deep, 3))] * 2,
+        scratch_shapes=[pltpu.VMEM((deep, FF, B), f32), pltpu.VMEM((deep, B, FF), f32)]
+        + [pltpu.VMEM((deep, D, B), f32)] * 2 + [pltpu.VMEM((deep, B, D), f32), pltpu.VMEM((D, 6 * D), bf16)]
+        + [pltpu.SemaphoreType.DMA((deep, 3))] * 2,
         compiler_params=pltpu.CompilerParams(vmem_limit_bytes=63 * MIB),
-        name="finish")(decay, *[t.reshape(TRI, B) for t in tris], *prods, s_up_old, a_down_old, *smalls,
-                       a_up_old, s_down_old, inv_u, inv_q)
+        name="finish")(decay, *[t.reshape(TRI, B) for t in tris], *prods, *smalls, a_up_old, s_down_old, inv_u, inv_q)
 
 
 def solution(mesh):
@@ -815,41 +860,43 @@
         wide_out, small_out, tri_out = (WIDE, f32, "w"), (SMALL, f32, "w"), ((TRI, B), f32, "w")
         long_out, short_out = ((FF, total), bf16, "cf"), ((D, total), bf16, "cb")
         board = Board()
+        decay = jnp.stack((factor_decay, jnp.float32(inv_n)))
+        board.arrays["decay"] = decay
         pre0, u1, ad0, au0, sd1 = run_stage(
-            board, stage1, "stage1", tile, [0.0] * (steps + 1),
-            ((tok, "rf"), (grad, "rf"), (w_up, 0), (w_down, 0), (tok, "rb"), (grad, "rb")),
-            (long_out, short_out, tri_out, small_out, small_out), acts + [w_t, pltpu.VMEM((D, FF), bf16)], 5 * unit, 0)
-        board.add("ad0", "tri", ad0)
+            board, stage1, "stage1", 2 * tile, [0.0] * (steps // 2),
+            ((tok, "r"), (grad, "r"), (w_up, 0), (w_down, 0)),
+            (long_out, ((D, total), bf16, "c"), tri_out, small_out, small_out),
+            [pltpu.VMEM((FF, 2 * tile), bf16), w_t, pltpu.VMEM((D, FF), bf16)], 5 * unit, 0)
+        board.add("ad0", "tri", ad0, a_down_old, 0)
         board.add("au0", "small", au0)
         board.add("sd1", "small", sd1)
         pre1, ad1, au1, dwd1 = run_stage(
-            board, stage2, "stage2", tile, [2.0] + [3.5] * steps, ((u1, "cf"), (w_up, 1), (u1, "cb"), (grad, "rb")),
+            board, stage2, "stage2", tile, [2.4] + [4.0] * steps, ((u1, "cf"), (w_up, 1), (u1, "cb"), (grad, "rb")),
             (long_out, tri_out, small_out, wide_out), acts + [w_t], 5 * unit, 1)
-        board.add("ad1", "tri", ad1)
+        board.add("ad1", "tri", ad1, a_down_old, 1)
         board.add("au1", "small", au1)
         board.add("dwd1", "wide", dwd1, a_down_inv, 1)
         e1, su1, dwu1 = run_stage(
-            board, stage3, "stage3", tile, [2.0] + [4.1] * steps,
+            board, stage3, "stage3", tile, [2.4] + [4.8] * steps,
             ((pre1, "cf"), (grad, "rf"), (w_down, 1), (w_up, 1), (u1, "cb")), (short_out, tri_out, wide_out), acts, 6 * unit, 2)
-        board.add("su1", "tri", su1)
+        board.add("su1", "tri", su1, s_up_old, 1)
         board.add("dwu1", "wide", dwu1, s_up_inv, 1)
         g0, sd0, dwd0, dwu0 = run_stage(
-            board, stage4, "stage4", tile, [2.0] + [3.1] * steps,
+            board, stage4, "stage4", tile, [2.5] + [3.6] * steps,
             ((pre0, "cf"), (e1, "cf"), (w_down, 0), (tok, "rb"), (e1, "cb")),
             (long_out, small_out, wide_out, wide_out), acts * 2, 4 * unit, 3)
         board.add("sd0", "small", sd0)
         board.add("dwd0", "wide", dwd0, a_down_inv, 0)
         board.add("dwu0", "wide", dwu0, s_up_inv, 0)
-        su0, = run_stage(board, stage5, "stage5", tile, [1.9] * steps, ((g0, "c"),), (tri_out,), [], 3 * unit, 4)
-        board.add("su0", "tri", su0)
+        su0, = run_stage(board, stage5, "stage5", tile, [2.2] * steps, ((g0, "c"),), (tri_out,), [], 3 * unit, 4)
+        board.add("su0", "tri", su0, s_up_old, 0)
         run_stage(board, None, "tail", tile, [0.1], (), (), [], unit, 5, last=True)
         done = board.arrays
-        decay = jnp.stack((factor_decay, jnp.float32(inv_n)))
         new_s, new_a, p_up, p_down, new_u, new_q = finish(
             decay, [done[n + ":dst"] for n in ("ad0", "ad1", "su0", "su1")],
             [done[n + ":dst"] for n in ("au0", "au1", "sd0", "sd1")],
             [done[n + ":dst"] for n in ("dwu0", "dwu1", "dwd0", "dwd1")],
-            s_up_old, a_down_old, a_up_old, s_down_old, a_up_inv, s_down_inv)
+            s_up_old, a_up_old, s_down_old, a_up_inv, s_down_inv)
         return p_up, p_down, new_u, new_s, new_a, new_q
 
     batch_spec = P("data", None)

time: 475 us -> 475 us (level)
    pallas_call x1, Pallas kernels: 42.1 us -> 35.2 us  [finish(): pl.pallas_call(final_kernel, in_specs=[SCALARS] + [ANY] * 8 + [vmem] * 8,...]
    pallas_call x6, Pallas kernels: 425 us -> 432 us  [run_stage(): pl.pallas_call(kernel, grid=(steps,), in_specs=[spec(kind, arr.shape) for...]
where the time goes in v1:
time: 475 us; the launch traced here: 469 us
  Pallas kernels  467 us (98%)
    pallas_call x6, Pallas kernels, run_stage(): pl.pallas_call(kernel, grid=(steps,), in_specs=[spec(kind, arr.shape) for...  432 us
    pallas_call x1, Pallas kernels, finish(): pl.pallas_call(final_kernel, in_specs=[SCALARS] + [ANY] * 8 + [vmem] * 8,...  35.2 us

profile of v1, /device:TPU:0, one launch (start us, length us, event | category | flops | bytes accessed | tf_op | source)
XLA Modules:
  0.0 469.4 jit_solution(9350012013566333183)
XLA Ops:
  1.3 0.7 pad_maximum_fusion.refs_5_.refs_6_.refs_4_.decay
  1.9 60.4 %stage1.1 = (bf16[1536,8192]{1,0:T(8,128)(2,1)}, bf16[384,8192]{1,0:T(8,128)(2,1)}, f32[5376,256]{1,0:T(8,128)}, f32[2,128,384]{2,1,0:T(8,128)}, f32[2,128,384]{2,1,0:T(8,128)}) custom-call(bf16[8192,384]{1,0:T(8,128)(2,1)} %refs_3_.7, bf16[8192,384]{1,0:T(8,128)(2,1)} %refs_1_.5, bf16[2,384,1536]{2,1,0:T(8,128)(2,1)} %refs_3_.6, bf16[2,1536,384]{2,1,0:T(8,128)(2,1)} %refs_2_.5), custom_call_target="tpu_custom_call" | custom-call | flops 48318382080 | bytes 41943040 | tf_op jit(solution)/shard_map/stage1/pallas_call | solution.py:741
  62.4 79.9 %stage2.1 = (bf16[1536,8192]{1,0:T(8,128)(2,1)}, f32[5376,256]{1,0:T(8,128)}, f32[2,128,384]{2,1,0:T(8,128)}, f32[2,384,768]{2,1,0:T(8,128)}, f32[2,2688,256]{2,...) custom-call(bf16[384,8192]{1,0:T(8,128)(2,1)} %get-tuple-element.62.refs_0_.refs_2_.refs_4_, ...), custom_call_target="tpu_custom_call" | custom-call | flops 48318382080 | bytes 41943040 | tf_op jit(solution)/shard_map/stage2/pallas_call | solution.py:741
  142.3 92.1 %stage3.1 = (bf16[384,8192]{1,0:T(8,128)(2,1)}, f32[5376,256]{1,0:T(8,128)}, f32[2,384,768]{2,1,0:T(8,128)}, f32[2,2688,256]{2,1,0:T(8,128)}, f32[2,128,384]{2,1...) custom-call(bf16[1536,8192]{1,0:T(8,128)(2,1)} %get-tuple-element.66, ...), custom_call_target="tpu_custom_call", output_to_operand_aliasing={{3}: (10, {}), {4}: (11, {}), {5}: (12, {})} | custom-call | flops 57982058496 | bytes 41943040 | tf_op jit(solution)/shard_map/stage3/pallas_call | solution.py:741
  234.5 74.2 %stage4.1 = (bf16[1536,8192]{1,0:T(8,128)(2,1)}, f32[2,128,384]{2,1,0:T(8,128)}, f32[2,384,768]{2,1,0:T(8,128)}, f32[2,384,768]{2,1,0:T(8,128)}, f32[2,2688,256]...) custom-call(bf16[1536,8192]{1,0:T(8,128)(2,1)} %get-tuple-element.74, ...), custom_call_target="tpu_custom_call", output_to_operand_aliasing={{4}: (13, {}), {5}: (14, {})} | custom-call | flops 38654705664 | bytes 41943040 | tf_op jit(solution)/shard_map/stage4/pallas_call | solution.py:741
  308.7 46.2 %stage5.1 = (f32[5376,256]{1,0:T(8,128)}, f32[2,2688,256]{2,1,0:T(8,128)}, f32[8,384]{1,0:T(8,128)}, f32[8,768]{1,0:T(8,128)}, f32[8,768]{1,0:T(8,128)}, /*index...) custom-call(bf16[1536,8192]{1,0:T(8,128)(2,1)} %get-tuple-element.84, ...), custom_call_target="tpu_custom_call", output_to_operand_aliasing={{1}: (8, {})} | custom-call | flops 28991029248 | bytes 41943040 | tf_op jit(solution)/shard_map/stage5/pallas_call | solution.py:741
  354.9 79.0 %tail.1 = (f32[2,2688,256]{2,1,0:T(8,128)}, f32[2,128,384]{2,1,0:T(8,128)}, f32[8,768]{1,0:T(8,128)}, f32[8,768]{1,0:T(8,128)}, f32[2,384,768]{2,1,0:T(8,128)}, ...) custom-call(f32[8,384]{1,0:T(8,128)} %get-tuple-element.92.refs_0_, ...), custom_call_target="tpu_custom_call", output_to_operand_aliasing={{0}: (12, {}), {4}: (13, {})} | custom-call | flops 9663676416 | bytes 41943040 | tf_op jit(solution)/shard_map/tail/pallas_call | solution.py:741
  433.9 35.2 %finish.1 = (f32[2,1536,1536]{2,1,0:T(8,128)}, f32[2,1536,1536]{2,1,0:T(8,128)}, f32[2,384,1536]{2,1,0:T(8,128)}, f32[2,1536,384]{2,1,0:T(8,128)}, f32[2,384,384]{2,1,0:T(8,128)}, /*index=5*/f32[2,384,384]{2,1,0:T(8,128)}) custom-call(f32[2]{0:T(128)} %pad_maximum_fusion.refs_5_.refs_6_.refs_4_.decay, f32[5376,256]{1,0:T(8,128)} %bitcast.13, ...), custom_call_target="tpu_custom_call" | custom-call | tf_op jit(solution)/shard_map/finish/pallas_call | solution.py:836

commit v2 on v1

--- a/solution.py
+++ b/solution.py
@@ -63,10 +63,10 @@
 
 
 MESH = pl.DeviceIdType.MESH
-ORDER_X, ORDER_Y, ORDER_Z, ORDER_A, ORDER_B = (
-    tuple(map(int, order)) for order in ("1234", "2134", "3412", "1342", "2341"))
+ORDERS = {key: tuple(map(int, order)) for key, order in
+          (("X", "1234"), ("Y", "2134"), ("Z", "3412"), ("A", "1342"), ("B", "2341"), ("C", "3421"))}
 LINKS = {0: {0: 6e5}, 1: {1: 45e3}, 2: {2: 45e3}, 3: {3: 45e3}, 4: {3: 45e3, 4: 23e3}}
-LAG = 2.5
+LAG = 2.0
 SLACK = 3.0
 
 
@@ -150,7 +150,7 @@
         if a < 5:
             work, recv = scr[3:5]
         elif a == 5:
-            work = named[self.name + ":first"].at[pl.ds(self.shard_row, 8), :] if self.wide else scr[3]
+            work = named[self.name + ":first"].at[pl.ds(self.shard_row, self.kept(5)), :] if self.wide else scr[3]
         sends, begin_recv, locals_ = {}, {}, []
 
         def remote(s, x, y):
@@ -280,7 +280,7 @@
         copies, swaps = [], []
         for i, flow in enumerate(self.flows):
             rows = named.get(flow.part + ":out", named.get(flow.part + ":in"))
-            spot = pl.ds(flow.shard_row, 8)
+            spot = pl.ds(flow.shard_row, flow.kept(5))
             copies.append(pltpu.make_async_copy(rows, own.at[spot, :], sem_l.at[i]))
             swaps.append(pltpu.make_async_remote_copy(
                 src_ref=rows, dst_ref=other.at[spot, :], send_sem=sem_s.at[i], recv_sem=sem_r.at[i],
@@ -301,7 +301,7 @@
         return {"begin": begin, "go": go}
 
 
-def plan(flows, firsts, tick_us, last, over=4.0):
+def plan(flows, firsts, tick_us, last, over=2.0):
     times = [0.0]
     for us in tick_us:
         times.append(times[-1] + us)
@@ -587,19 +587,20 @@
 SMALL = (2, 128, 384)
 WIDE = (2, 384, 768)
 TRI_SHAPE = (2, TRI // 2, B)
-FORMS = {
-    "tri": (TRI_SHAPE, ((512, ORDER_X), (512, ORDER_B), (512, ORDER_X), (512, ORDER_Z), (512, ORDER_Y), (128, ORDER_B))),
-    "wide": (WIDE, ((128, ORDER_Y), (128, ORDER_Y), (128, ORDER_A))),
-    "small": (SMALL, ((128, ORDER_X),)),
+CUTS = {
+    "ad0": "128X,1024X,512Y,512Z,512A", "au0": "128Z", "sd1": "128X",
+    "ad1": "512X,128Y,512C,512Y,512A,512X", "au1": "128Z", "dwd1": "128X,256B",
+    "su1": "512X,128X,512B,1024Y,512X", "dwu1": "256X,128C",
+    "sd0": "128X", "dwd0": "128Z,256X", "dwu0": "256X,128B", "su0": "512C,512X,128Y,512B,512X,512Y",
 }
-
-
-def flows_of(name, form):
-    shape, cuts = FORMS[form]
+FORMS = {"tri": TRI_SHAPE, "wide": WIDE, "small": SMALL}
+
+
+def flows_of(name, form, cuts):
     flows, row = [], 0
-    for rows, order in cuts:
-        flows.append(Flow(name, row, rows, shape[2], order, row // 16, form == "wide"))
-        row += rows
+    for cut in cuts.split(","):
+        flows.append(Flow(name, row, int(cut[:-1]), FORMS[form][2], ORDERS[cut[-1]], row // 16, form == "wide"))
+        row += flows[-1].rows
     return flows
 
 
@@ -645,10 +646,10 @@
     def __init__(self):
         self.flows, self.firsts, self.arrays, self.forms, self.fresh = [], [], {}, {}, 0
 
-    def add(self, name, form, array, other=None, block=0):
-        flows = flows_of(name, form)
+    def add(self, name, form, cuts, array, other=None, block=0):
+        flows = flows_of(name, form, cuts)
         self.flows += flows
-        self.forms[name] = FORMS[form][0]
+        self.forms[name] = FORMS[form]
         self.arrays[name + ":src"] = array.reshape(self.forms[name])
         if form == "wide":
             self.firsts.append(First(name, flows, other, block))
@@ -867,29 +868,29 @@
             ((tok, "r"), (grad, "r"), (w_up, 0), (w_down, 0)),
             (long_out, ((D, total), bf16, "c"), tri_out, small_out, small_out),
             [pltpu.VMEM((FF, 2 * tile), bf16), w_t, pltpu.VMEM((D, FF), bf16)], 5 * unit, 0)
-        board.add("ad0", "tri", ad0, a_down_old, 0)
-        board.add("au0", "small", au0)
-        board.add("sd1", "small", sd1)
+        board.add("ad0", "tri", CUTS["ad0"], ad0, a_down_old, 0)
+        board.add("au0", "small", CUTS["au0"], au0)
+        board.add("sd1", "small", CUTS["sd1"], sd1)
         pre1, ad1, au1, dwd1 = run_stage(
-            board, stage2, "stage2", tile, [2.4] + [4.0] * steps, ((u1, "cf"), (w_up, 1), (u1, "cb"), (grad, "rb")),
+            board, stage2, "stage2", tile, [2.2] + [3.47] * steps, ((u1, "cf"), (w_up, 1), (u1, "cb"), (grad, "rb")),
             (long_out, tri_out, small_out, wide_out), acts + [w_t], 5 * unit, 1)
-        board.add("ad1", "tri", ad1, a_down_old, 1)
-        board.add("au1", "small", au1)
-        board.add("dwd1", "wide", dwd1, a_down_inv, 1)
+        board.add("ad1", "tri", CUTS["ad1"], ad1, a_down_old, 1)
+        board.add("au1", "small", CUTS["au1"], au1)
+        board.add("dwd1", "wide", CUTS["dwd1"], dwd1, a_down_inv, 1)
         e1, su1, dwu1 = run_stage(
-            board, stage3, "stage3", tile, [2.4] + [4.8] * steps,
+            board, stage3, "stage3", tile, [2.4] + [4.4] * steps,
             ((pre1, "cf"), (grad, "rf"), (w_down, 1), (w_up, 1), (u1, "cb")), (short_out, tri_out, wide_out), acts, 6 * unit, 2)
-        board.add("su1", "tri", su1, s_up_old, 1)
-        board.add("dwu1", "wide", dwu1, s_up_inv, 1)
+        board.add("su1", "tri", CUTS["su1"], su1, s_up_old, 1)
+        board.add("dwu1", "wide", CUTS["dwu1"], dwu1, s_up_inv, 1)
         g0, sd0, dwd0, dwu0 = run_stage(
-            board, stage4, "stage4", tile, [2.5] + [3.6] * steps,
+            board, stage4, "stage4", tile, [2.2] + [3.2] * steps,
             ((pre0, "cf"), (e1, "cf"), (w_down, 0), (tok, "rb"), (e1, "cb")),
             (long_out, small_out, wide_out, wide_out), acts * 2, 4 * unit, 3)
-        board.add("sd0", "small", sd0)
-        board.add("dwd0", "wide", dwd0, a_down_inv, 0)
-        board.add("dwu0", "wide", dwu0, s_up_inv, 0)
-        su0, = run_stage(board, stage5, "stage5", tile, [2.2] * steps, ((g0, "c"),), (tri_out,), [], 3 * unit, 4)
-        board.add("su0", "tri", su0, s_up_old, 0)
+        board.add("sd0", "small", CUTS["sd0"], sd0)
+        board.add("dwd0", "wide", CUTS["dwd0"], dwd0, a_down_inv, 0)
+        board.add("dwu0", "wide", CUTS["dwu0"], dwu0, s_up_inv, 0)
+        su0, = run_stage(board, stage5, "stage5", tile, [1.84] * steps, ((g0, "c"),), (tri_out,), [], 3 * unit, 4)
+        board.add("su0", "tri", CUTS["su0"], su0, s_up_old, 0)
         run_stage(board, None, "tail", tile, [0.1], (), (), [], unit, 5, last=True)
         done = board.arrays
         new_s, new_a, p_up, p_down, new_u, new_q = finish(

time: 475 us -> 470 us (0.989)
  Pallas kernels: 467 us -> 462 us
    pallas_call x6, Pallas kernels: 432 us -> 427 us  [run_stage(): pl.pallas_call(kernel, grid=(steps,), in_specs=[spec(kind, arr.shape) for...]
where the time goes in v2:
time: 470 us; the launch traced here: 464 us
  Pallas kernels  462 us (98%)
    pallas_call x6, Pallas kernels, run_stage(): pl.pallas_call(kernel, grid=(steps,), in_specs=[spec(kind, arr.shape) for...  427 us
    pallas_call x1, Pallas kernels, finish(): pl.pallas_call(final_kernel, in_specs=[SCALARS] + [ANY] * 8 + [vmem] * 8,...  35.3 us

profile of v2, /device:TPU:0, one launch (start us, length us, event | category | flops | bytes accessed | tf_op | source)
XLA Modules:
  0.0 464.1 jit_solution(6758670534077430666)
XLA Ops:
  1.3 0.6 pad_maximum_fusion.refs_5_.refs_6_.decay
  1.9 60.4 %stage1.1 = (bf16[1536,8192]{1,0:T(8,128)(2,1)}, bf16[384,8192]{1,0:T(8,128)(2,1)}, f32[5376,256]{1,0:T(8,128)}, f32[2,128,384]{2,1,0:T(8,128)}, f32[2,128,384]{2,1,0:T(8,128)}) custom-call(bf16[8192,384]{1,0:T(8,128)(2,1)} %refs_3_.7, bf16[8192,384]{1,0:T(8,128)(2,1)} %refs_1_.5, bf16[2,384,1536]{2,1,0:T(8,128)(2,1)} %refs_3_.6, bf16[2,1536,384]{2,1,0:T(8,128)(2,1)} %refs_2_.5), custom_call_target="tpu_custom_call" | custom-call | flops 48318382080 | bytes 41943040 | tf_op jit(solution)/shard_map/stage1/pallas_call | solution.py:742
  62.3 77.4 %stage2.1 = (bf16[1536,8192]{1,0:T(8,128)(2,1)}, f32[5376,256]{1,0:T(8,128)}, f32[2,128,384]{2,1,0:T(8,128)}, f32[2,384,768]{2,1,0:T(8,128)}, f32[2,2688,256]{2,...) custom-call(bf16[384,8192]{1,0:T(8,128)(2,1)} %get-tuple-element.63.refs_0_.refs_2_.refs_4_, ...), custom_call_target="tpu_custom_call" | custom-call | flops 48318382080 | bytes 41943040 | tf_op jit(solution)/shard_map/stage2/pallas_call | solution.py:742
  139.7 90.6 %stage3.1 = (bf16[384,8192]{1,0:T(8,128)(2,1)}, f32[5376,256]{1,0:T(8,128)}, f32[2,384,768]{2,1,0:T(8,128)}, f32[2,2688,256]{2,1,0:T(8,128)}, f32[2,128,384]{2,1...) custom-call(bf16[1536,8192]{1,0:T(8,128)(2,1)} %get-tuple-element.67, ...), custom_call_target="tpu_custom_call", output_to_operand_aliasing={{3}: (10, {}), {4}: (11, {}), {5}: (12, {})} | custom-call | flops 57982058496 | bytes 41943040 | tf_op jit(solution)/shard_map/stage3/pallas_call | solution.py:742
  230.3 72.3 %stage4.1 = (bf16[1536,8192]{1,0:T(8,128)(2,1)}, f32[2,128,384]{2,1,0:T(8,128)}, f32[2,384,768]{2,1,0:T(8,128)}, f32[2,384,768]{2,1,0:T(8,128)}, f32[2,128,384]{...) custom-call(bf16[1536,8192]{1,0:T(8,128)(2,1)} %get-tuple-element.75, ...), custom_call_target="tpu_custom_call", output_to_operand_aliasing={{4}: (12, {}), {5}: (13, {}), {6}: (14, {})} | custom-call | flops 38654705664 | bytes 41943040 | tf_op jit(solution)/shard_map/stage4/pallas_call | solution.py:742
  302.6 37.8 %stage5.1 = (f32[5376,256]{1,0:T(8,128)}, f32[2,2688,256]{2,1,0:T(8,128)}, f32[2,2688,256]{2,1,0:T(8,128)}, f32[16,768]{1,0:T(8,128)}, f32[2,384,768]{2,1,0:T(8,...) custom-call(bf16[1536,8192]{1,0:T(8,128)(2,1)} %get-tuple-element.84, ...), custom_call_target="tpu_custom_call", output_to_operand_aliasing={{1}: (7, {}), {2}: (8, {}), {4}: (9, {})} | custom-call | flops 28991029248 | bytes 41943040 | tf_op jit(solution)/shard_map/stage5/pallas_call | solution.py:742
  340.4 88.1 %tail.1 = (f32[2,2688,256]{2,1,0:T(8,128)}, f32[2,128,384]{2,1,0:T(8,128)}, f32[8,768]{1,0:T(8,128)}, f32[16,768]{1,0:T(8,128)}, f32[16,768]{1,0:T(8,128)}, /*in...) custom-call(f32[16,384]{1,0:T(8,128)} %get-tuple-element.95.refs_0_,, ...), custom_call_target="tpu_custom_call", output_to_operand_aliasing={{0}: (13, {})} | custom-call | flops 9663676416 | bytes 41943040 | tf_op jit(solution)/shard_map/tail/pallas_call | solution.py:742
  428.5 35.3 %finish.1 = (f32[2,1536,1536]{2,1,0:T(8,128)}, f32[2,1536,1536]{2,1,0:T(8,128)}, f32[2,384,1536]{2,1,0:T(8,128)}, f32[2,1536,384]{2,1,0:T(8,128)}, f32[2,384,384]{2,1,0:T(8,128)}, /*index=5*/f32[2,384,384]{2,1,0:T(8,128)}) custom-call(f32[2]{0:T(128)} %pad_maximum_fusion.refs_5_.refs_6_.decay, f32[5376,256]{1,0:T(8,128)} %bitcast.13, f32[5376,256]{1,0:T(8,128)} %bitcast.11, ...), custom_call_target="tpu_custom_call" | custom-call | tf_op jit(solution)/shard_map/finish/pallas_call | solution.py:837

commit v3 on v2

--- a/solution.py
+++ b/solution.py
@@ -66,7 +66,7 @@
 ORDERS = {key: tuple(map(int, order)) for key, order in
           (("X", "1234"), ("Y", "2134"), ("Z", "3412"), ("A", "1342"), ("B", "2341"), ("C", "3421"))}
 LINKS = {0: {0: 6e5}, 1: {1: 45e3}, 2: {2: 45e3}, 3: {3: 45e3}, 4: {3: 45e3, 4: 23e3}}
-LAG = 2.0
+LAG = 1.5
 SLACK = 3.0
 
 
@@ -83,12 +83,13 @@
     return bits, [me + (1 - 2 * bits[d]) * (1 << d) for d in range(5)]
 
 
-def entry_barrier():
-    peers = my_bits()[1]
-    barrier = pltpu.get_barrier_semaphore()
-    for peer in peers:
-        pl.semaphore_signal(barrier, inc=1, device_id=(peer,), device_id_type=MESH)
-    pl.semaphore_wait(barrier, len(peers))
+def enter():
+    for peer in my_bits()[1]:
+        pl.semaphore_signal(pltpu.get_barrier_semaphore(), inc=1, device_id=(peer,), device_id_type=MESH)
+
+
+def await_peers():
+    pl.semaphore_wait(pltpu.get_barrier_semaphore(), 5)
 
 
 def al(row):
@@ -414,7 +415,8 @@
                             out.append((x, "go", 5))
 
     for t, now in enumerate(times[:-1]):
-        sweep(now, slots[t])
+        if t or last:
+            sweep(now, slots[t])
     now = times[-1]
     while True:
         sweep(now, rest)
@@ -532,7 +534,7 @@
     def dot(k):
         return mm(up_s[block(k), :], u_t[...], NN)
 
-    wide = [functools.partial(add_wide, dwd, grad_b, hid_s, TT, h) for h in range(2)]
+    wide = [functools.partial(add_wide, dwd, grad_b, hid_s, TT, h) for h in PAIR]
     backs = tri_pieces(tri, hid_s, wide[:1], (wide[1], lambda: add_small_nt(small_u, u_b)))
     staged(dot, gelu_act(pre_out, new_s), backs, ((hid_s, new_s),), (tri, small_u, dwd), setup)
 
@@ -550,7 +552,7 @@
     def up():
         err_out[...] = mm(w_up[0], g_s[...], NN).astype(bf16)
 
-    wide = [functools.partial(add_wide, dwu, u_b, g_s, NT, h) for h in range(2)]
+    wide = [functools.partial(add_wide, dwu, u_b, g_s, NT, h) for h in PAIR]
     staged(dot, act, tri_pieces(tri, g_s, wide, (up,)), ((g_s, new_s),), (tri, dwu))
 
 
@@ -574,7 +576,7 @@
         else:
             dwu[h, :, :] += mm(tok_b[...], g_s[h * FF // 2:(h + 1) * FF // 2, :], TT)
 
-    backs = [functools.partial(part, q, h) for q in range(2) for h in range(2)]
+    backs = [functools.partial(part, q, h) for q in PAIR for h in PAIR]
     backs += [lambda: add_small_nt(small_q, err_b), lambda: None]
     staged(dot, act, backs, ((hid_s, new_h), (g_s, new_g)), (small_q, dwd, dwu))
 
@@ -588,10 +590,10 @@
 WIDE = (2, 384, 768)
 TRI_SHAPE = (2, TRI // 2, B)
 CUTS = {
-    "ad0": "128X,1024X,512Y,512Z,512A", "au0": "128Z", "sd1": "128X",
-    "ad1": "512X,128Y,512C,512Y,512A,512X", "au1": "128Z", "dwd1": "128X,256B",
-    "su1": "512X,128X,512B,1024Y,512X", "dwu1": "256X,128C",
-    "sd0": "128X", "dwd0": "128Z,256X", "dwu0": "256X,128B", "su0": "512C,512X,128Y,512B,512X,512Y",
+    "ad0": "512Z,512A,128C,1024A,512X", "au0": "128X", "sd1": "128Y",
+    "ad1": "128X,1024Y,512C,1024X", "au1": "128Z", "dwd1": "384Y",
+    "su1": "512C,512X,128X,512X,512X,512Y", "dwu1": "128Y,256X",
+    "sd0": "128Z", "dwd0": "128B,256X", "dwu0": "256Y,128C", "su0": "128X,512X,512X,512C,512X,512B",
 }
 FORMS = {"tri": TRI_SHAPE, "wide": WIDE, "small": SMALL}
 
@@ -638,6 +640,7 @@
     return pl.BlockSpec((1,) + shape[1:], lambda i: (b, 0, 0), pipeline_mode=pl.Buffered(1))
 
 
+PAIR = range(2)
 ANY = pl.BlockSpec(memory_space=pl.ANY)
 SCALARS = pl.BlockSpec(memory_space=pltpu.SMEM)
 
@@ -717,7 +720,8 @@
         step = pl.program_id(0)
         events = {}
         if moving:
-            pl.when(step == 0)(entry_barrier)
+            pl.when(step == 0)(enter)
+            pl.when(step == min(1, steps - 1))(await_peers)
         for job, s in zip(runs + moving, scr):
             events[job] = job.bind(named, pull(len(s)))
 
@@ -754,8 +758,10 @@
     return values[:n_out]
 
 
-def final_kernel(decay, t0, t1, t2, t3, n0, n1, n2, n3, s0, s1, s2, s3, old_u, old_q, inv_u, inv_q,
-                 new_s, new_a, p_up, p_down, new_u, new_q, pk, tr, nv, pv, pt, inv_s, sem_in, sem_out):
+def final_kernel(decay, t0, t1, t2, t3, n0, n1, n2, n3, *refs):
+    small_in, small_out, outs, scratch = refs[:8], refs[12:14], refs[8:12], refs[14:]
+    new_s, new_a, p_up, p_down = outs
+    pk, tr, nv, pv, pt, inv_s, sums, olds, invs, news, sem_in, sem_out, sem_small = scratch
     rho = decay[0]
     scale = (1.0 - rho) * decay[1]
     deep = pk.shape[0]
@@ -786,28 +792,47 @@
             parts.append((tr.at[s, :, pl.ds(0, j * B)], new.at[b, pl.ds(j * B, B), pl.ds(0, j * B)]))
         return [pltpu.make_async_copy(x, y, sem_out.at[s, i]) for i, (x, y) in enumerate(parts)]
 
+    places = [sums.at[i] for i in range(4)] + [olds.at[i] for i in PAIR] + [invs.at[i] for i in PAIR]
+    early = [pltpu.make_async_copy(x, y, sem_small.at[i]) for i, (x, y) in enumerate(zip(small_in, places))]
+    late = [pltpu.make_async_copy(news.at[i], small_out[i], sem_small.at[len(early) + i]) for i in PAIR]
+
+    def mix_small():
+        h = B // 2
+        for c in early[:6]:
+            c.wait()
+        for i in range(4):
+            acc, old, new = sums.at[i], olds.at[i // 2, i % 2], news.at[i // 2, i % 2]
+            top = rho * old[:h, :] + scale * acc[0]
+            mid = rho * old[h:B, h:] + scale * acc[1, :, :B]
+            low = rho * old[B:, B:] + scale * acc[1, :, B:]
+            new[:h, :] = top
+            new[h:B, h:] = mid
+            new[B:, B:] = low
+            new[h:, :h] = top[:, h:].T
+            new[B:, h:B] = mid[:, h:].T
+        for c in late:
+            c.start()
+
+    for c in early[6:]:
+        c.start()
     for u in range(ahead):
         for c in loads(u):
             c.start()
-    h = B // 2
-    for acc, old, new, b in ((s0, old_u, new_u, 0), (s1, old_u, new_u, 1), (s2, old_q, new_q, 0), (s3, old_q, new_q, 1)):
-        top = rho * old[b, :h, :] + scale * acc[0]
-        mid = rho * old[b, h:B, h:] + scale * acc[1, :, :B]
-        low = rho * old[b, B:, B:] + scale * acc[1, :, B:]
-        new[b, :h, :] = top
-        new[b, h:B, h:] = mid
-        new[b, B:, B:] = low
-        new[b, h:, :h] = top[:, h:].T
-        new[b, B:, h:B] = mid[:, h:].T
+    for c in early[:6]:
+        c.start()
     for u, (q, src, new, b, j, off, n) in enumerate(units):
         s = u % deep
         for c in loads(u):
             c.wait()
+        if u == NB:
+            mix_small()
+        if j == 0 and b == 0:
+            early[6 + q // 2].wait()
         for i in range(j):
             here = slice(i * B, (i + 1) * B)
             tr[s, :, here] = pk[s, here, :].T
         if j == 0:
-            x, y, z = thirds((inv_u if q < 2 else inv_q)[b])
+            x, y, z = thirds(invs[q // 2, b])
             for i, third in enumerate((x, x, y, x, y, z)):
                 inv_s[:, i * D:(i + 1) * D] = third
         x, y, z = thirds(nv[s])
@@ -824,24 +849,26 @@
                     c.wait()
             for c in loads(u + ahead):
                 c.start()
+    for c in late:
+        c.wait()
     for u in range(len(units) - deep, len(units)):
         for c in stores(u):
             c.wait()
 
 
 def finish(decay, tris, smalls, prods, s_up_old, a_up_old, s_down_old, inv_u, inv_q):
-    vmem = pl.BlockSpec(memory_space=pltpu.VMEM)
     big = jax.ShapeDtypeStruct(s_up_old.shape, f32)
     small = jax.ShapeDtypeStruct(a_up_old.shape, f32)
     deep = 6
     return pl.pallas_call(
         final_kernel,
-        in_specs=[SCALARS] + [ANY] * 8 + [vmem] * 8,
-        out_specs=[ANY] * 4 + [vmem] * 2,
+        in_specs=[SCALARS] + [ANY] * 16,
+        out_specs=[ANY] * 6,
         out_shape=[big, big, jax.ShapeDtypeStruct((2, D, FF), f32), jax.ShapeDtypeStruct((2, FF, D), f32), small, small],
         scratch_shapes=[pltpu.VMEM((deep, FF, B), f32), pltpu.VMEM((deep, B, FF), f32)]
         + [pltpu.VMEM((deep, D, B), f32)] * 2 + [pltpu.VMEM((deep, B, D), f32), pltpu.VMEM((D, 6 * D), bf16)]
-        + [pltpu.SemaphoreType.DMA((deep, 3))] * 2,
+        + [pltpu.VMEM((4,) + SMALL, f32)] + [pltpu.VMEM((2,) + a_up_old.shape, f32)] * 3
+        + [pltpu.SemaphoreType.DMA((deep, 3))] * 2 + [pltpu.SemaphoreType.DMA((10,))],
         compiler_params=pltpu.CompilerParams(vmem_limit_bytes=63 * MIB),
         name="finish")(decay, *[t.reshape(TRI, B) for t in tris], *prods, *smalls, a_up_old, s_down_old, inv_u, inv_q)
 
@@ -872,7 +899,7 @@
         board.add("au0", "small", CUTS["au0"], au0)
         board.add("sd1", "small", CUTS["sd1"], sd1)
         pre1, ad1, au1, dwd1 = run_stage(
-            board, stage2, "stage2", tile, [2.2] + [3.47] * steps, ((u1, "cf"), (w_up, 1), (u1, "cb"), (grad, "rb")),
+            board, stage2, "stage2", tile, [2.2] + [3.36] * steps, ((u1, "cf"), (w_up, 1), (u1, "cb"), (grad, "rb")),
             (long_out, tri_out, small_out, wide_out), acts + [w_t], 5 * unit, 1)
         board.add("ad1", "tri", CUTS["ad1"], ad1, a_down_old, 1)
         board.add("au1", "small", CUTS["au1"], au1)
@@ -889,7 +916,7 @@
         board.add("sd0", "small", CUTS["sd0"], sd0)
         board.add("dwd0", "wide", CUTS["dwd0"], dwd0, a_down_inv, 0)
         board.add("dwu0", "wide", CUTS["dwu0"], dwu0, s_up_inv, 0)
-        su0, = run_stage(board, stage5, "stage5", tile, [1.84] * steps, ((g0, "c"),), (tri_out,), [], 3 * unit, 4)
+        su0, = run_stage(board, stage5, "stage5", tile, [1.75] * steps, ((g0, "c"),), (tri_out,), [], 3 * unit, 4)
         board.add("su0", "tri", CUTS["su0"], su0, s_up_old, 0)
         run_stage(board, None, "tail", tile, [0.1], (), (), [], unit, 5, last=True)
         done = board.arrays

time: 470 us -> 466 us (level)
  no operation moved by 1% of the time
where the time goes in v3:
time: 466 us; the launch traced here: 460 us
  Pallas kernels  458 us (98%)
    pallas_call x6, Pallas kernels, run_stage(): pl.pallas_call(kernel, grid=(steps,), in_specs=[spec(kind, arr.shape) for...  425 us
    pallas_call x1, Pallas kernels, finish(): pl.pallas_call(final_kernel, in_specs=[SCALARS] + [ANY] * 16, out_specs=[...  33.5 us

profile of v3, /device:TPU:0, one launch (start us, length us, event | category | flops | bytes accessed | tf_op | source)
XLA Modules:
  0.0 460.4 jit_solution(14817191853398490786)
XLA Ops:
  1.3 0.6 pad_maximum_fusion.refs_5_.refs_6_.decay
  1.9 60.4 %stage1.1 = (bf16[1536,8192]{1,0:T(8,128)(2,1)}, bf16[384,8192]{1,0:T(8,128)(2,1)}, f32[5376,256]{1,0:T(8,128)}, f32[2,128,384]{2,1,0:T(8,128)}, f32[2,128,384]{2,1,0:T(8,128)}) custom-call(bf16[8192,384]{1,0:T(8,128)(2,1)} %refs_3_.7, bf16[8192,384]{1,0:T(8,128)(2,1)} %refs_1_.5, bf16[2,384,1536]{2,1,0:T(8,128)(2,1)} %refs_3_.6, bf16[2,1536,384]{2,1,0:T(8,128)(2,1)} %refs_2_.5), custom_call_target="tpu_custom_call" | custom-call | flops 48318382080 | bytes 41943040 | tf_op jit(solution)/shard_map/stage1/pallas_call | solution.py:746
  62.3 76.1 %stage2.1 = (bf16[1536,8192]{1,0:T(8,128)(2,1)}, f32[5376,256]{1,0:T(8,128)}, f32[2,128,384]{2,1,0:T(8,128)}, f32[2,384,768]{2,1,0:T(8,128)}, f32[2,2688,256]{2,...) custom-call(bf16[384,8192]{1,0:T(8,128)(2,1)} %get-tuple-element.60.refs_0_.refs_2_.refs_4_, ...), custom_call_target="tpu_custom_call" | custom-call | flops 48318382080 | bytes 41943040 | tf_op jit(solution)/shard_map/stage2/pallas_call | solution.py:746
  138.4 86.7 %stage3.1 = (bf16[384,8192]{1,0:T(8,128)(2,1)}, f32[5376,256]{1,0:T(8,128)}, f32[2,384,768]{2,1,0:T(8,128)}, f32[2,2688,256]{2,1,0:T(8,128)}, f32[2,128,384]{2,1...) custom-call(bf16[1536,8192]{1,0:T(8,128)(2,1)} %get-tuple-element.64, ...), custom_call_target="tpu_custom_call", output_to_operand_aliasing={{3}: (10, {}), {4}: (11, {}), {5}: (12, {})} | custom-call | flops 57982058496 | bytes 41943040 | tf_op jit(solution)/shard_map/stage3/pallas_call | solution.py:746
  225.2 71.9 %stage4.1 = (bf16[1536,8192]{1,0:T(8,128)(2,1)}, f32[2,128,384]{2,1,0:T(8,128)}, f32[2,384,768]{2,1,0:T(8,128)}, f32[2,384,768]{2,1,0:T(8,128)}, f32[2,2688,256]...) custom-call(bf16[1536,8192]{1,0:T(8,128)(2,1)} %get-tuple-element.72, ...), custom_call_target="tpu_custom_call", output_to_operand_aliasing={{4}: (11, {}), {5}: (12, {})} | custom-call | flops 38654705664 | bytes 41943040 | tf_op jit(solution)/shard_map/stage4/pallas_call | solution.py:746
  297.1 35.6 %stage5.1 = (f32[5376,256]{1,0:T(8,128)}, f32[2,2688,256]{2,1,0:T(8,128)}, f32[2,2688,256]{2,1,0:T(8,128)}, f32[16,768]{1,0:T(8,128)}, f32[32,384]{1,0:T(8,128)}...) custom-call(bf16[1536,8192]{1,0:T(8,128)(2,1)} %get-tuple-element.79, ...), custom_call_target="tpu_custom_call", output_to_operand_aliasing={{1}: (6, {}), {2}: (7, {})} | custom-call | flops 28991029248 | bytes 41943040 | tf_op jit(solution)/shard_map/stage5/pallas_call | solution.py:746
  332.7 93.8 %tail.1 = (f32[2,2688,256]{2,1,0:T(8,128)}, f32[2,384,768]{2,1,0:T(8,128)}, f32[2,128,384]{2,1,0:T(8,128)}, f32[8,768]{1,0:T(8,128)}, f32[16,768]{1,0:T(8,128)},...) custom-call(f32[32,384]{1,0:T(8,128)} %get-tuple-element.88.refs_0_,, ...), custom_call_target="tpu_custom_call", output_to_operand_aliasing={{0}: (13, {}), {1}: (14, {})} | custom-call | flops 9663676416 | bytes 41943040 | tf_op jit(solution)/shard_map/tail/pallas_call | solution.py:746
  426.6 33.5 %finish.1 = (f32[2,1536,1536]{2,1,0:T(8,128)}, f32[2,1536,1536]{2,1,0:T(8,128)}, f32[2,384,1536]{2,1,0:T(8,128)}, f32[2,1536,384]{2,1,0:T(8,128)}, f32[2,384,384]{2,1,0:T(8,128)}, /*index=5*/f32[2,384,384]{2,1,0:T(8,128)}) custom-call(f32[2]{0:T(128)} %pad_maximum_fusion.refs_5_.refs_6_.decay, f32[5376,256]{1,0:T(8,128)} %bitcast.13, f32[5376,256]{1,0:T(8,128)} %bitcast.12, ...), custom_call_target="tpu_custom_call" | custom-call | tf_op jit(solution)/shard_map/finish/pallas_call | solution.py:863

commit v4 on v3

--- a/solution.py
+++ b/solution.py
@@ -66,7 +66,7 @@
 ORDERS = {key: tuple(map(int, order)) for key, order in
           (("X", "1234"), ("Y", "2134"), ("Z", "3412"), ("A", "1342"), ("B", "2341"), ("C", "3421"))}
 LINKS = {0: {0: 6e5}, 1: {1: 45e3}, 2: {2: 45e3}, 3: {3: 45e3}, 4: {3: 45e3, 4: 23e3}}
-LAG = 1.5
+LAG = 2.0
 SLACK = 3.0
 
 
@@ -556,7 +556,7 @@
     staged(dot, act, tri_pieces(tri, g_s, wide, (up,)), ((g_s, new_s),), (tri, dwu))
 
 
-def stage4(pre_in, err_t, w_down, tok_b, err_b, g_out, small_q, dwd, dwu, new_h, hid_s, new_g, g_s):
+def stage4(pre_in, err_t, w_down, tok_b, err_b, tri, small_q, dwd, dwu, new_h, hid_s, new_g, g_s):
     def dot(k):
         return mm(w_down[0, block(k), :], err_t[...], NN)
 
@@ -566,34 +566,22 @@
         sig, cubic = half_sig(pre)
         hid, slope = gelu_back(pre, sig, cubic)
         new_h[block(k), :] = hid.astype(bf16)
-        grad_up = (d_hid * slope).astype(bf16)
-        new_g[block(k), :] = grad_up
-        g_out[block(k), :] = grad_up
-
-    def part(q, h):
-        if q:
-            dwd[h, :, :] += mm(err_b[...], hid_s[h * FF // 2:(h + 1) * FF // 2, :], NT)
-        else:
-            dwu[h, :, :] += mm(tok_b[...], g_s[h * FF // 2:(h + 1) * FF // 2, :], TT)
-
-    backs = [functools.partial(part, q, h) for q in PAIR for h in PAIR]
-    backs += [lambda: add_small_nt(small_q, err_b), lambda: None]
-    staged(dot, act, backs, ((hid_s, new_h), (g_s, new_g)), (small_q, dwd, dwu))
-
-
-def stage5(g_in, tri):
-    zero_first((tri,))
-    add_tri(tri, g_in)
+        new_g[block(k), :] = (d_hid * slope).astype(bf16)
+
+    downs = [functools.partial(add_wide, dwd, err_b, hid_s, NT, h) for h in PAIR]
+    ups = [functools.partial(add_wide, dwu, tok_b, g_s, TT, h) for h in PAIR]
+    backs = tri_pieces(tri, g_s, downs, ups + [lambda: add_small_nt(small_q, err_b)])
+    staged(dot, act, backs, ((hid_s, new_h), (g_s, new_g)), (tri, small_q, dwd, dwu))
 
 
 SMALL = (2, 128, 384)
 WIDE = (2, 384, 768)
 TRI_SHAPE = (2, TRI // 2, B)
 CUTS = {
-    "ad0": "512Z,512A,128C,1024A,512X", "au0": "128X", "sd1": "128Y",
-    "ad1": "128X,1024Y,512C,1024X", "au1": "128Z", "dwd1": "384Y",
-    "su1": "512C,512X,128X,512X,512X,512Y", "dwu1": "128Y,256X",
-    "sd0": "128Z", "dwd0": "128B,256X", "dwu0": "256Y,128C", "su0": "128X,512X,512X,512C,512X,512B",
+    "ad0": "1024X,512A,1024Y,128B", "au0": "128X", "sd1": "128Y",
+    "ad1": "128A,1024A,512B,512Y,512Y", "au1": "128Y", "dwd1": "128Y,256A",
+    "su1": "128A,512B,512X,512X,512A,512Y", "dwu1": "384Y",
+    "sd0": "128Y", "dwd0": "256B,128Z", "dwu0": "128Y,256X", "su0": "512A,512Y,512C,512X,128Z,512X",
 }
 FORMS = {"tri": TRI_SHAPE, "wide": WIDE, "small": SMALL}
 
@@ -899,26 +887,25 @@
         board.add("au0", "small", CUTS["au0"], au0)
         board.add("sd1", "small", CUTS["sd1"], sd1)
         pre1, ad1, au1, dwd1 = run_stage(
-            board, stage2, "stage2", tile, [2.2] + [3.36] * steps, ((u1, "cf"), (w_up, 1), (u1, "cb"), (grad, "rb")),
+            board, stage2, "stage2", tile, [2.2] + [3.5] * steps, ((u1, "cf"), (w_up, 1), (u1, "cb"), (grad, "rb")),
             (long_out, tri_out, small_out, wide_out), acts + [w_t], 5 * unit, 1)
         board.add("ad1", "tri", CUTS["ad1"], ad1, a_down_old, 1)
         board.add("au1", "small", CUTS["au1"], au1)
         board.add("dwd1", "wide", CUTS["dwd1"], dwd1, a_down_inv, 1)
         e1, su1, dwu1 = run_stage(
-            board, stage3, "stage3", tile, [2.4] + [4.4] * steps,
+            board, stage3, "stage3", tile, [2.4] + [4.22] * steps,
             ((pre1, "cf"), (grad, "rf"), (w_down, 1), (w_up, 1), (u1, "cb")), (short_out, tri_out, wide_out), acts, 6 * unit, 2)
         board.add("su1", "tri", CUTS["su1"], su1, s_up_old, 1)
         board.add("dwu1", "wide", CUTS["dwu1"], dwu1, s_up_inv, 1)
-        g0, sd0, dwd0, dwu0 = run_stage(
-            board, stage4, "stage4", tile, [2.2] + [3.2] * steps,
+        su0, sd0, dwd0, dwu0 = run_stage(
+            board, stage4, "stage4", tile, [2.4] + [4.4] * steps,
             ((pre0, "cf"), (e1, "cf"), (w_down, 0), (tok, "rb"), (e1, "cb")),
-            (long_out, small_out, wide_out, wide_out), acts * 2, 4 * unit, 3)
+            (tri_out, small_out, wide_out, wide_out), acts * 2, 7 * unit, 3)
         board.add("sd0", "small", CUTS["sd0"], sd0)
         board.add("dwd0", "wide", CUTS["dwd0"], dwd0, a_down_inv, 0)
         board.add("dwu0", "wide", CUTS["dwu0"], dwu0, s_up_inv, 0)
-        su0, = run_stage(board, stage5, "stage5", tile, [1.75] * steps, ((g0, "c"),), (tri_out,), [], 3 * unit, 4)
         board.add("su0", "tri", CUTS["su0"], su0, s_up_old, 0)
-        run_stage(board, None, "tail", tile, [0.1], (), (), [], unit, 5, last=True)
+        run_stage(board, None, "tail", tile, [0.1], (), (), [], unit, 4, last=True)
         done = board.arrays
         new_s, new_a, p_up, p_down, new_u, new_q = finish(
             decay, [done[n + ":dst"] for n in ("ad0", "ad1", "su0", "su1")],

time: 466 us -> 463 us (level)
    pallas_call x6 -> x5, Pallas kernels: 425 us -> 422 us  [run_stage(): pl.pallas_call(kernel, grid=(steps,), in_specs=[spec(kind, arr.shape) for...]
where the time goes in v4:
time: 463 us; the launch traced here: 457 us
  Pallas kernels  455 us (98%)
    pallas_call x5, Pallas kernels, run_stage(): pl.pallas_call(kernel, grid=(steps,), in_specs=[spec(kind, arr.shape) for...  422 us
    pallas_call x1, Pallas kernels, finish(): pl.pallas_call(final_kernel, in_specs=[SCALARS] + [ANY] * 16, out_specs=[...  33.2 us

profile of v4, /device:TPU:0, one launch (start us, length us, event | category | flops | bytes accessed | tf_op | source)
XLA Modules:
  0.0 457.5 jit_solution(1139889250280549832)
XLA Ops:
  1.3 0.6 pad_maximum_fusion.refs_5_.refs_6_.refs_4_.decay
  1.9 60.4 %stage1.1 = (bf16[1536,8192]{1,0:T(8,128)(2,1)}, bf16[384,8192]{1,0:T(8,128)(2,1)}, f32[5376,256]{1,0:T(8,128)}, f32[2,128,384]{2,1,0:T(8,128)}, f32[2,128,384]{2,1,0:T(8,128)}) custom-call(bf16[8192,384]{1,0:T(8,128)(2,1)} %refs_3_.7, bf16[8192,384]{1,0:T(8,128)(2,1)} %refs_1_.5, bf16[2,384,1536]{2,1,0:T(8,128)(2,1)} %refs_3_.6, bf16[2,1536,384]{2,1,0:T(8,128)(2,1)} %refs_2_.5), custom_call_target="tpu_custom_call" | custom-call | flops 48318382080 | bytes 41943040 | tf_op jit(solution)/shard_map/stage1/pallas_call | solution.py:734
  62.3 74.0 %stage2.1 = (bf16[1536,8192]{1,0:T(8,128)(2,1)}, f32[5376,256]{1,0:T(8,128)}, f32[2,128,384]{2,1,0:T(8,128)}, f32[2,384,768]{2,1,0:T(8,128)}, f32[2,2688,256]{2,...) custom-call(bf16[384,8192]{1,0:T(8,128)(2,1)} %get-tuple-element.54.refs_0_.refs_2_.refs_4_, ...), custom_call_target="tpu_custom_call" | custom-call | flops 48318382080 | bytes 41943040 | tf_op jit(solution)/shard_map/stage2/pallas_call | solution.py:734
  136.4 88.1 %stage3.1 = (bf16[384,8192]{1,0:T(8,128)(2,1)}, f32[5376,256]{1,0:T(8,128)}, f32[2,384,768]{2,1,0:T(8,128)}, f32[2,2688,256]{2,1,0:T(8,128)}, f32[2,128,384]{2,1...) custom-call(bf16[1536,8192]{1,0:T(8,128)(2,1)} %get-tuple-element.58, ...), custom_call_target="tpu_custom_call", output_to_operand_aliasing={{3}: (10, {}), {4}: (11, {}), {5}: (12, {})} | custom-call | flops 57982058496 | bytes 41943040 | tf_op jit(solution)/shard_map/stage3/pallas_call | solution.py:734
  224.5 92.5 %stage4.1 = (f32[5376,256]{1,0:T(8,128)}, f32[2,128,384]{2,1,0:T(8,128)}, f32[2,384,768]{2,1,0:T(8,128)}, f32[2,384,768]{2,1,0:T(8,128)}, f32[2,2688,256]{2,1,0:...) custom-call(bf16[1536,8192]{1,0:T(8,128)(2,1)} %get-tuple-element.53, ...), custom_call_target="tpu_custom_call", output_to_operand_aliasing={{4}: (12, {}), {5}: (13, {}), {6}: (14, {}), {7}: (15, {}),... | custom-call | flops 67645734912 | bytes 41943040 | tf_op jit(solution)/shard_map/stage4/pallas_call | solution.py:734
  317.0 107.0 %tail.1 = (f32[2,2688,256]{2,1,0:T(8,128)}, f32[2,384,768]{2,1,0:T(8,128)}, f32[2,128,384]{2,1,0:T(8,128)}, f32[16,768]{1,0:T(8,128)}, f32[8,768]{1,0:T(8,128)},...) custom-call(f32[2,128,384]{2,1,0:T(8,128)} %get-tuple-element.77.ref, ...), custom_call_target="tpu_custom_call", output_to_operand_aliasing={{0}: (10, {}), {1}: (11, {})} | custom-call | flops 9663676416 | bytes 41943040 | tf_op jit(solution)/shard_map/tail/pallas_call | solution.py:734
  424.0 33.2 %finish.1 = (f32[2,1536,1536]{2,1,0:T(8,128)}, f32[2,1536,1536]{2,1,0:T(8,128)}, f32[2,384,1536]{2,1,0:T(8,128)}, f32[2,1536,384]{2,1,0:T(8,128)}, f32[2,384,384]{2,1,0:T(8,128)}, /*index=5*/f32[2,384,384]{2,1,0:T(8,128)}) custom-call(f32[2]{0:T(128)} %pad_maximum_fusion.refs_5_.refs_6_.refs_4_.decay, f32[5376,256]{1,0:T(8,128)} %bitcast.13, ...), custom_call_target="tpu_custom_call" | custom-call | tf_op jit(solution)/shard_map/finish/pallas_call | solution.py:851

commit v5 on v4

--- a/solution.py
+++ b/solution.py
@@ -67,7 +67,7 @@
           (("X", "1234"), ("Y", "2134"), ("Z", "3412"), ("A", "1342"), ("B", "2341"), ("C", "3421"))}
 LINKS = {0: {0: 6e5}, 1: {1: 45e3}, 2: {2: 45e3}, 3: {3: 45e3}, 4: {3: 45e3, 4: 23e3}}
 LAG = 2.0
-SLACK = 3.0
+SLACK = 4.0
 
 
 def PRIORITY(f):
@@ -205,7 +205,7 @@
         def mix():
             rho = named["decay"][0]
             x, y = pl.ds(al(offs[4] - base), lens[4]), pl.ds(begin_recv[4], lens[4])
-            total = (work[x, :] + recv[y, :]) * named["decay"][1]
+            total = (work[x, :] + recv[y, :]) * named["scale"]
             work[x, :] = rho * scr[5][...] + (1.0 - rho) * total
 
         def take(s, then):
@@ -302,7 +302,7 @@
         return {"begin": begin, "go": go}
 
 
-def plan(flows, firsts, tick_us, last, over=2.0):
+def plan(flows, firsts, tick_us, last, over=0.0):
     times = [0.0]
     for us in tick_us:
         times.append(times[-1] + us)
@@ -578,10 +578,10 @@
 WIDE = (2, 384, 768)
 TRI_SHAPE = (2, TRI // 2, B)
 CUTS = {
-    "ad0": "1024X,512A,1024Y,128B", "au0": "128X", "sd1": "128Y",
-    "ad1": "128A,1024A,512B,512Y,512Y", "au1": "128Y", "dwd1": "128Y,256A",
-    "su1": "128A,512B,512X,512X,512A,512Y", "dwu1": "384Y",
-    "sd0": "128Y", "dwd0": "256B,128Z", "dwu0": "128Y,256X", "su0": "512A,512Y,512C,512X,128Z,512X",
+    "ad0": "128B,1024A,1024X,512C", "au0": "128Z", "sd1": "128Y",
+    "ad1": "512X,1024Y,512Z,128Z,512Y", "au1": "128Z", "dwd1": "256X,128Y",
+    "su1": "512B,128A,512A,512Y,512X,512B", "dwu1": "384Y",
+    "sd0": "128X", "dwd0": "128C,128B,128Y", "dwu0": "256X,128B", "su0": "512A,128Y,512A,512Y,512X,512Z",
 }
 FORMS = {"tri": TRI_SHAPE, "wide": WIDE, "small": SMALL}
 
@@ -634,8 +634,10 @@
 
 
 class Board:
-    def __init__(self):
-        self.flows, self.firsts, self.arrays, self.forms, self.fresh = [], [], {}, {}, 0
+    def __init__(self, decay, scale):
+        self.flows, self.firsts, self.arrays, self.forms = [], [], {}, {}
+        self.scale = scale
+        self.arrays["decay"] = decay
 
     def add(self, name, form, cuts, array, other=None, block=0):
         flows = flows_of(name, form, cuts)
@@ -704,7 +706,7 @@
 
         c_in, m_in, c_out, m_out, c_scr = pull(n_in), pull(n_min), pull(n_out), pull(n_mout), pull(n_scr)
         named = dict(zip(m_ins, m_in))
-        named.update(zip(m_outs, m_out))
+        named.update(zip(m_outs, m_out), scale=board.scale)
         step = pl.program_id(0)
         events = {}
         if moving:
@@ -746,12 +748,12 @@
     return values[:n_out]
 
 
-def final_kernel(decay, t0, t1, t2, t3, n0, n1, n2, n3, *refs):
+def final_kernel(mean, decay, t0, t1, t2, t3, n0, n1, n2, n3, *refs):
     small_in, small_out, outs, scratch = refs[:8], refs[12:14], refs[8:12], refs[14:]
     new_s, new_a, p_up, p_down = outs
     pk, tr, nv, pv, pt, inv_s, sums, olds, invs, news, sem_in, sem_out, sem_small = scratch
     rho = decay[0]
-    scale = (1.0 - rho) * decay[1]
+    scale = (1.0 - rho) * mean
     deep = pk.shape[0]
     ahead = deep // 2
     units = []
@@ -824,7 +826,7 @@
             for i, third in enumerate((x, x, y, x, y, z)):
                 inv_s[:, i * D:(i + 1) * D] = third
         x, y, z = thirds(nv[s])
-        prod = mm(inv_s[...], jnp.concatenate((x, y, x, z, y, x), axis=0), NN) * decay[1]
+        prod = mm(inv_s[...], jnp.concatenate((x, y, x, z, y, x), axis=0), NN) * mean
         if q < 2:
             pv[s] = prod
         else:
@@ -844,12 +846,12 @@
             c.wait()
 
 
-def finish(decay, tris, smalls, prods, s_up_old, a_up_old, s_down_old, inv_u, inv_q):
+def finish(mean, decay, tris, smalls, prods, s_up_old, a_up_old, s_down_old, inv_u, inv_q):
     big = jax.ShapeDtypeStruct(s_up_old.shape, f32)
     small = jax.ShapeDtypeStruct(a_up_old.shape, f32)
     deep = 6
     return pl.pallas_call(
-        final_kernel,
+        functools.partial(final_kernel, mean),
         in_specs=[SCALARS] + [ANY] * 16,
         out_specs=[ANY] * 6,
         out_shape=[big, big, jax.ShapeDtypeStruct((2, D, FF), f32), jax.ShapeDtypeStruct((2, FF, D), f32), small, small],
@@ -875,9 +877,8 @@
         unit = 2 * total * FF * D
         wide_out, small_out, tri_out = (WIDE, f32, "w"), (SMALL, f32, "w"), ((TRI, B), f32, "w")
         long_out, short_out = ((FF, total), bf16, "cf"), ((D, total), bf16, "cb")
-        board = Board()
-        decay = jnp.stack((factor_decay, jnp.float32(inv_n)))
-        board.arrays["decay"] = decay
+        decay = factor_decay.reshape(1)
+        board = Board(decay, inv_n)
         pre0, u1, ad0, au0, sd1 = run_stage(
             board, stage1, "stage1", 2 * tile, [0.0] * (steps // 2),
             ((tok, "r"), (grad, "r"), (w_up, 0), (w_down, 0)),
@@ -887,18 +888,18 @@
         board.add("au0", "small", CUTS["au0"], au0)
         board.add("sd1", "small", CUTS["sd1"], sd1)
         pre1, ad1, au1, dwd1 = run_stage(
-            board, stage2, "stage2", tile, [2.2] + [3.5] * steps, ((u1, "cf"), (w_up, 1), (u1, "cb"), (grad, "rb")),
+            board, stage2, "stage2", tile, [2.2] + [3.85] * steps, ((u1, "cf"), (w_up, 1), (u1, "cb"), (grad, "rb")),
             (long_out, tri_out, small_out, wide_out), acts + [w_t], 5 * unit, 1)
         board.add("ad1", "tri", CUTS["ad1"], ad1, a_down_old, 1)
         board.add("au1", "small", CUTS["au1"], au1)
         board.add("dwd1", "wide", CUTS["dwd1"], dwd1, a_down_inv, 1)
         e1, su1, dwu1 = run_stage(
-            board, stage3, "stage3", tile, [2.4] + [4.22] * steps,
+            board, stage3, "stage3", tile, [2.4] + [4.5] * steps,
             ((pre1, "cf"), (grad, "rf"), (w_down, 1), (w_up, 1), (u1, "cb")), (short_out, tri_out, wide_out), acts, 6 * unit, 2)
         board.add("su1", "tri", CUTS["su1"], su1, s_up_old, 1)
         board.add("dwu1", "wide", CUTS["dwu1"], dwu1, s_up_inv, 1)
         su0, sd0, dwd0, dwu0 = run_stage(
-            board, stage4, "stage4", tile, [2.4] + [4.4] * steps,
+            board, stage4, "stage4", tile, [2.5] + [4.65] * steps,
             ((pre0, "cf"), (e1, "cf"), (w_down, 0), (tok, "rb"), (e1, "cb")),
             (tri_out, small_out, wide_out, wide_out), acts * 2, 7 * unit, 3)
         board.add("sd0", "small", CUTS["sd0"], sd0)
@@ -908,7 +909,7 @@
         run_stage(board, None, "tail", tile, [0.1], (), (), [], unit, 4, last=True)
         done = board.arrays
         new_s, new_a, p_up, p_down, new_u, new_q = finish(
-            decay, [done[n + ":dst"] for n in ("ad0", "ad1", "su0", "su1")],
+            inv_n, decay, [done[n + ":dst"] for n in ("ad0", "ad1", "su0", "su1")],
             [done[n + ":dst"] for n in ("au0", "au1", "sd0", "sd1")],
             [done[n + ":dst"] for n in ("dwu0", "dwu1", "dwd0", "dwd1")],
             s_up_old, a_up_old, s_down_old, a_up_inv, s_down_inv)

time: 463 us -> 459 us (level)
  no operation moved by 1% of the time
where the time goes in v5:
time: 459 us; the launch traced here: 453 us
  Pallas kernels  451 us (98%)
    pallas_call x5, Pallas kernels, run_stage(): pl.pallas_call(kernel, grid=(steps,), in_specs=[spec(kind, arr.shape) for...  419 us
    pallas_call x1, Pallas kernels, finish(): pl.pallas_call(functools.partial(final_kernel, mean), in_specs=[SCALARS]...  32.5 us

profile of v5, /device:TPU:0, one launch (start us, length us, event | category | flops | bytes accessed | tf_op | source)
XLA Modules:
  0.0 452.9 jit_solution(13235697760349768737)
XLA Ops:
  1.3 60.5 %stage1.1 = (bf16[1536,8192]{1,0:T(8,128)(2,1)}, bf16[384,8192]{1,0:T(8,128)(2,1)}, f32[5376,256]{1,0:T(8,128)}, f32[2,128,384]{2,1,0:T(8,128)}, f32[2,128,384]{2,1,0:T(8,128)}) custom-call(bf16[8192,384]{1,0:T(8,128)(2,1)} %refs_3_.7, bf16[8192,384]{1,0:T(8,128)(2,1)} %refs_1_.5, bf16[2,384,1536]{2,1,0:T(8,128)(2,1)} %refs_3_.6, bf16[2,1536,384]{2,1,0:T(8,128)(2,1)} %refs_2_.5), custom_call_target="tpu_custom_call" | custom-call | flops 48318382080 | bytes 41943040 | tf_op jit(solution)/shard_map/stage1/pallas_call | solution.py:736
  61.8 74.0 %stage2.1 = (bf16[1536,8192]{1,0:T(8,128)(2,1)}, f32[5376,256]{1,0:T(8,128)}, f32[2,128,384]{2,1,0:T(8,128)}, f32[2,384,768]{2,1,0:T(8,128)}, f32[2,2688,256]{2,...) custom-call(bf16[384,8192]{1,0:T(8,128)(2,1)} %get-tuple-element.51.refs_0_.refs_2_.refs_4_, ...), custom_call_target="tpu_custom_call" | custom-call | flops 48318382080 | bytes 41943040 | tf_op jit(solution)/shard_map/stage2/pallas_call | solution.py:736
  135.8 86.3 %stage3.1 = (bf16[384,8192]{1,0:T(8,128)(2,1)}, f32[5376,256]{1,0:T(8,128)}, f32[2,384,768]{2,1,0:T(8,128)}, f32[2,2688,256]{2,1,0:T(8,128)}, f32[2,128,384]{2,1...) custom-call(bf16[1536,8192]{1,0:T(8,128)(2,1)} %get-tuple-element.55, ...), custom_call_target="tpu_custom_call", output_to_operand_aliasing={{3}: (11, {}), {4}: (12, {}), {5}: (13, {})} | custom-call | flops 57982058496 | bytes 41943040 | tf_op jit(solution)/shard_map/stage3/pallas_call | solution.py:736
  222.2 91.8 %stage4.1 = (f32[5376,256]{1,0:T(8,128)}, f32[2,128,384]{2,1,0:T(8,128)}, f32[2,384,768]{2,1,0:T(8,128)}, f32[2,384,768]{2,1,0:T(8,128)}, f32[2,2688,256]{2,1,0:...) custom-call(bf16[1536,8192]{1,0:T(8,128)(2,1)} %get-tuple-element.64, ...), custom_call_target="tpu_custom_call", output_to_operand_aliasing={{4}: (12, {}), {5}: (13, {})} | custom-call | flops 67645734912 | bytes 41943040 | tf_op jit(solution)/shard_map/stage4/pallas_call | solution.py:736
  314.0 106.1 %tail.1 = (f32[2,128,384]{2,1,0:T(8,128)}, f32[2,2688,256]{2,1,0:T(8,128)}, f32[2,128,384]{2,1,0:T(8,128)}, f32[8,768]{1,0:T(8,128)}, f32[8,768]{1,0:T(8,128)}, ...) custom-call(f32[2,128,384]{2,1,0:T(8,128)} %get-tuple-element.73.ref, ...), custom_call_target="tpu_custom_call", output_to_operand_aliasing={{0}: (10, {}), {1}: (11, {})} | custom-call | flops 9663676416 | bytes 41943040 | tf_op jit(solution)/shard_map/tail/pallas_call | solution.py:736
  420.1 32.5 %finish.1 = (f32[2,1536,1536]{2,1,0:T(8,128)}, f32[2,1536,1536]{2,1,0:T(8,128)}, f32[2,384,1536]{2,1,0:T(8,128)}, f32[2,1536,384]{2,1,0:T(8,128)}, f32[2,384,384]{2,1,0:T(8,128)}, /*index=5*/f32[2,384,384]{2,1,0:T(8,128)}) custom-call(f32[1]{0:T(128)} %bitcast.13.decay, f32[5376,256]{1,0:T(8,128)} %bitcast.17, f32[5376,256]{1,0:T(8,128)} %bitcast.16, ...), custom_call_target="tpu_custom_call" | custom-call | tf_op jit(solution)/shard_map/finish/pallas_call | solution.py:853
